TPU v7x, 256 devices: a whole 4x4x8 slice. The times are simulated.
256 devices in a mesh: param: 32 (over z, x), task: 8 (over y, core).
Axes of the slice: x: 4, y: 4, z: 8, core: 2. Of those that a mesh axis runs over, the one named last changes fastest.
Arguments:
- task_ids: int32 [1024], P('task'), may hold values from 0 to 2047
- task_table: bfloat16 [2048, 256], P('param'), may hold values from -12 to 12
- enc_in: bfloat16 [256, 512], replicated, may hold values from -0.375 to 0.375
- enc_out: bfloat16 [512, 256], replicated, may hold values from -0.25 to 0.25
- generator: bfloat16 [256, 8, 114688], P(None, None, ('param', 'task')), may hold values from -6 to 6
- gain: bfloat16 [8, 114688], P(None, ('param', 'task')), may hold values from 0.099609375 to 1.8984375
Outputs:
- adapters: bfloat16 [1024, 8, 114688], P(None, None, ('param', 'task'))
Inputs may be any that keep to these rules, and one draw needn't show every extreme that they name: `task_ids`: each id names a row of task_table.
All inputs are finite; a program needn't handle non-finite values.
Results may differ from a plain program's by a relative error of at most 0.00055.
The roundings to bfloat16 on the way count: a program that leaves them out, or rounds other values in their place, can miss the bound.
Values may be sent and summed in bfloat16 or wider, within the bound.
No kernel may reach another device: no remote copies, remote signals or barrier semaphores. Data moves between devices by JAX's collectives and lax.ppermute only.
A program may use at most 64 MiB of HBM per device.

v0:
```python
import jax
import jax.numpy as jnp
from jax import lax
from jax.sharding import Mesh
from jax.sharding import PartitionSpec as P

D = 3584
RANK = 32
PARAM = ("param_0", "param_1")
TASK = ("task_0", "task_1")
PARAM_TASK = ("param_0", "param_1", "task_0", "task_1")


EPSILON = 1e-06


def laid_out(tiles, dim):
    lengths = list(tiles.shape[1:])
    lengths[dim] *= tiles.shape[0]
    return jnp.moveaxis(tiles, 0, dim).reshape(lengths)


def copy_for_each(x, axis):
    copies = jnp.broadcast_to(x, (lax.axis_size(axis), *x.shape))
    return lax.all_to_all(copies, axis, split_axis=0, concat_axis=0, tiled=True)


def gathered_copies(x, axis, dim):
    return laid_out(copy_for_each(x, axis), dim)


def over_copies(x, axis):
    return copy_for_each(x, axis).sum(axis=0)


def by_axis(x, axes):
    far, near = axes
    return over_copies(over_copies(x, near), far)


def select_rows(wanted, table_part):
    labels = lax.broadcasted_iota(jnp.int32, (1, table_part.shape[0]), 1)
    one_hot = (wanted[:, None] == labels).astype(jnp.bfloat16)
    return jnp.dot(one_hot, table_part, preferred_element_type=jnp.float32)


def look_up(wanted, task_table):
    whole_table = gathered_copies(task_table, PARAM, 0)
    found = select_rows(wanted, whole_table).astype(jnp.bfloat16)
    return found


def encode(raw_rows, enc_in, enc_out):
    inner_act = jax.nn.gelu(jnp.dot(raw_rows, enc_in, preferred_element_type=jnp.float32)).astype(
        jnp.bfloat16
    )
    mixed_sum = raw_rows.astype(jnp.float32) + jnp.dot(
        inner_act, enc_out, preferred_element_type=jnp.float32
    )
    return mixed_sum.astype(jnp.bfloat16)


def on_device(task_ids, task_table, enc_in, enc_out, generator, gain):
    groups = generator.shape[1]
    columns = generator.shape[2]
    flat_weights = generator.reshape(generator.shape[0], groups * columns)
    every_id = lax.all_gather(task_ids, TASK, axis=0, tiled=True)
    embedded = encode(look_up(every_id, task_table), enc_in, enc_out)
    generated = jnp.dot(embedded, flat_weights, preferred_element_type=jnp.float32)
    generated = generated.reshape(generated.shape[0], groups, columns)
    squares = jnp.sum(generated * generated, axis=2)
    totals = by_axis(squares, ("param_0", ("param_1", "task_0", "task_1")))
    inverse = lax.rsqrt(totals / (D * RANK) + EPSILON)
    scaled = generated * inverse[:, :, None] * gain.astype(jnp.float32)[None, :, :]
    return scaled.astype(jnp.bfloat16)


def solution(mesh):
    torus = Mesh(mesh.devices.reshape(8, 4, 4, 2), ("param_0", "param_1", "task_0", "task_1"))
    return jax.shard_map(
        on_device,
        mesh=torus,
        in_specs=(
            P(TASK),
            P(PARAM, None),
            P(),
            P(),
            P(None, None, PARAM_TASK),
            P(None, PARAM_TASK),
        ),
        out_specs=P(None, None, PARAM_TASK),
        check_vma=False,
    )
```

profile of v0, /device:TPU:1, one launch (start us, length us, event | category | flops | bytes accessed | tf_op | source)
XLA Modules:
  0.0 105.5 jit_solution(1677882748042664104)
XLA Ops:
  0.0 0.0 copy-start
  0.0 0.0 copy-start.2
  0.0 2.0 %broadcast_in_dim.12 = bf16[32,64,256]{2,1,0:T(8,128)(2,1)} broadcast(bf16[64,256]{1,0:T(8,128)(2,1)} %param.7), dimensions={1,2} | broadcast | bytes 1081344 | tf_op jit(solution)/shard_map/broadcast_in_dim | solution.py:24
  2.0 11.9 %all-to-all-start = ((bf16[32,64,256]{2,1,0:T(8,128)(2,1)}), bf16[32,64,256]{2,1,0:T(8,128)(2,1)S(1)}, u32[]{:S(2)}, u32[]{:S(2)}) async-start(bf16[32,64,256]{2,1,0:T(8,128)(2,1)} %broadcast_in_dim.12), calls=%async_computation | async-start | bytes 2097152 | tf_op jit(solution)/shard_map/all_to_all | solution.py:25
  13.9 0.0 copy-done.2
  13.9 11.6 %all-gather = s32[8,1,128]{2,1,0:T(1,128)S(1)} all-gather(s32[1,1,128]{2,1,0:T(1,128)S(1)} %bitcast.21), channel_id=1, replica_groups=mesh['param_0'=8,'param_1'=4,'task_0'=4,'task_1'=2] {'task_0','task_1'}, dimensions={0}, use_global_device_ids=true | all-gather | bytes 4608 | tf_op jit(solution)/shard_map/all_gather | solution.py:67
  25.5 14.6 %all-to-all-done = bf16[32,64,256]{2,1,0:T(8,128)(2,1)S(1)} async-done(((bf16[32,64,256]{2,1,0:T(8,128)(2,1)}), bf16[32,64,256]{2,1,0:T(8,128)(2,1)S(1)}, u32[]{:S(2)}, u32[]{:S(2)}) %all-to-all-start) | async-done | bytes 1048608 | tf_op jit(solution)/shard_map/all_to_all | solution.py:25
  40.1 0.0 copy-start.3
  40.1 0.0 copy-start.4
  40.1 2.3 %fusion.15 = bf16[1024,256]{1,0:T(8,128)(2,1)} fusion(bf16[2048,256]{1,0:T(8,128)(2,1)S(1)} %bitcast.19, s32[1024]{0:T(1024)S(1)} %bitcast.20), kind=kOutput, calls=%fused_computation.19 | convolution fusion | flops 1076101120 | bytes 1576960 | tf_op jit(solution)/shard_map/dot_general | solution.py:44
  42.4 0.0 copy-done.3
  42.4 0.0 copy-done.4
  42.4 2.2 %fusion.16 = bf16[1024,256,1]{1,0,2:T(8,128)(2,1)S(1)} fusion(bf16[512,256]{1,0:T(8,128)(2,1)S(1)} %copy-done.3, bf16[1024,256]{1,0:T(8,128)(2,1)} %fusion.15, bf16[256,512]{1,0:T(8,128)(2,1)S(1)} %copy-done.4), kind=kOutput, calls=%fused_computation.20 | convolution fusion | flops 542375936 | bytes 1572864 | tf_op jit(solution)/shard_map/dot_general | solution.py:57
  44.6 0.0 copy-done
  44.6 7.3 %multiply_reduce_fusion = (f32[1024,8]{0,1:T(8,128)S(1)}, f32[1024,8,448]{0,2,1:T(8,128)}) fusion(bf16[1024,256,1]{1,0,2:T(8,128)(2,1)S(1)} %fusion.16, bf16[256,8,448]{0,2,1:T(8,128)(2,1)S(1)} %copy-done), kind=kOutput, calls=%fused_computation.1 | convolution fusion | flops 1886380032 | bytes 17072128 | tf_op jit(solution)/shard_map/dot_general | solution.py:69
  51.9 0.1 broadcast_in_dim.13
  52.0 0.0 copy-start.1
  52.1 26.9 %all_to_all.15 = f32[32,1024,8]{1,2,0:T(8,128)S(1)} all-to-all(f32[32,1024,8]{1,2,0:T(8,128)S(1)} %broadcast_in_dim.13), channel_id=1, replica_groups=mesh['param_0'=8,'param_1'=4,'task_0'=4,'task_1'=2] {'param_1','task_0',..., dimensions={0} | all-to-all | bytes 2097152 | tf_op jit(solution)/shard_map/all_to_all | solution.py:25
  79.0 0.1 reduce_sum.28
  79.0 0.7 broadcast_in_dim.14
  79.7 3.4 %all-to-all-start.2 = ((f32[8,1024,8]{1,2,0:T(8,128)}), f32[8,1024,8]{1,2,0:T(8,128)S(1)}, u32[]{:S(2)}, u32[]{:S(2)}) async-start(f32[8,1024,8]{1,2,0:T(8,128)} %broadcast_in_dim.14), calls=%async_computation.2 | async-start | bytes 524288 | tf_op jit(solution)/shard_map/all_to_all | solution.py:25
  83.2 0.0 copy-done.1
  83.2 12.3 %all-to-all-done.2 = f32[8,1024,8]{1,2,0:T(8,128)S(1)} async-done(((f32[8,1024,8]{1,2,0:T(8,128)}), f32[8,1024,8]{1,2,0:T(8,128)S(1)}, u32[]{:S(2)}, u32[]{:S(2)}) %all-to-all-start.2) | async-done | bytes 262176 | tf_op jit(solution)/shard_map/all_to_all | solution.py:25
  95.5 10.0 %multiply_convert_fusion = bf16[1024,8,448]{0,2,1:T(8,128)(2,1)} fusion(f32[1024,8,448]{0,2,1:T(8,128)} %get-tuple-element.6, f32[8,448]{1,0:T(8,128)S(1)} %convert_element_type.23, f32[1024,8]{0,1:T(8,128)S(1)} %add_rsqrt_fusion), kind=kLoop, calls=%fused_computation | loop fusion | flops 11010048 | bytes 22067200 | tf_op jit(solution)/shard_map/convert_element_type | solution.py:75
  (3 shorter events, 0.0 us)
Async XLA Ops:
  0.0 44.6 %copy-start = (bf16[256,8,448]{0,2,1:T(8,128)(2,1)S(1)}, bf16[256,8,448]{0,2,1:T(8,128)(2,1)}, u32[]{:S(2)}) copy-start(bf16[256,8,448]{0,2,1:T(8,128)(2,1)} %param.10) | copy-start | bytes 5505028
  0.0 13.9 %copy-start.2 = (s32[128]{0:T(128)S(1)}, s32[128]{0:T(128)}, u32[]{:S(2)}) copy-start(s32[128]{0:T(128)} %param.6) | copy-start | bytes 1540
  2.0 38.1 %all-to-all-start = ((bf16[32,64,256]{2,1,0:T(8,128)(2,1)}), bf16[32,64,256]{2,1,0:T(8,128)(2,1)S(1)}, u32[]{:S(2)}, u32[]{:S(2)}) async-start(bf16[32,64,256]{2,1,0:T(8,128)(2,1)} %broadcast_in_dim.12), calls=%async_computation | async-start | bytes 2097152 | tf_op jit(solution)/shard_map/all_to_all | solution.py:25
  40.1 2.3 %copy-start.3 = (bf16[512,256]{1,0:T(8,128)(2,1)S(1)}, bf16[512,256]{1,0:T(8,128)(2,1)}, u32[]{:S(2)}) copy-start(bf16[512,256]{1,0:T(8,128)(2,1)} %param.9) | copy-start | bytes 786436
  40.1 2.3 %copy-start.4 = (bf16[256,512]{1,0:T(8,128)(2,1)S(1)}, bf16[256,512]{1,0:T(8,128)(2,1)}, u32[]{:S(2)}) copy-start(bf16[256,512]{1,0:T(8,128)(2,1)} %param.8) | copy-start | bytes 786436
  52.0 31.1 %copy-start.1 = (bf16[8,448]{1,0:T(8,128)(2,1)S(1)}, bf16[8,448]{1,0:T(8,128)(2,1)}, u32[]{:S(2)}) copy-start(bf16[8,448]{1,0:T(8,128)(2,1)} %param.11) | copy-start | bytes 21508
  79.7 15.7 %all-to-all-start.2 = ((f32[8,1024,8]{1,2,0:T(8,128)}), f32[8,1024,8]{1,2,0:T(8,128)S(1)}, u32[]{:S(2)}, u32[]{:S(2)}) async-start(f32[8,1024,8]{1,2,0:T(8,128)} %broadcast_in_dim.14), calls=%async_computation.2 | async-start | bytes 524288 | tf_op jit(solution)/shard_map/all_to_all | solution.py:25
where the time goes:
time: 106 us
  blocking collectives  38.5 us (36%)
  waiting for transfers between devices  26.9 us (25%)
  starting transfers between devices  15.3 us (14%)
  matrix products  11.9 us (11%)
  other arithmetic  10.1 us (10%)
  local copies, waits for them, and re-layouts  2.84 us (3%)
    all_to_all x1, blocking collectives, copy_for_each(): return lax.all_to_all(copies, axis, split_axis=0, concat_axis=0, tiled=True)  26.9 us
    all_to_all x2, waiting for transfers between devices, copy_for_each(): return lax.all_to_all(copies, axis, split_axis=0, concat_axis=0, tiled=True)  26.9 us
    all_to_all x2, starting transfers between devices, copy_for_each(): return lax.all_to_all(copies, axis, split_axis=0, concat_axis=0, tiled=True)  15.3 us
    all_gather x1, blocking collectives, on_device(): every_id = lax.all_gather(task_ids, TASK, axis=0, tiled=True)  11.6 us
    convert_element_type x1, other arithmetic, on_device(): return scaled.astype(jnp.bfloat16)  10 us
    dot_general x1, matrix products, on_device(): jnp.dot(embedded, flat_weights, preferred_element_type=jnp.float32)  7.32 us
    broadcast_in_dim x3, local copies, waits for them, and re-layouts, copy_for_each(): copies = jnp.broadcast_to(x, (lax.axis_size(axis), *x.shape))  2.82 us
    dot_general x1, matrix products, select_rows(): return jnp.dot(one_hot, table_part, preferred_element_type=jnp.float32)  2.3 us
  transfers between devices with their start and end apart: 2, of which 2 were waited for; matrix products, arithmetic and copies ran while one was open for 0% of the time, Pallas kernels for 0%

commit v1 on v0

v1 whole, which is shorter than its diff:
```python
import jax
import jax.numpy as jnp
from jax import lax
from jax.experimental import pallas as pl
from jax.experimental.pallas import tpu as pltpu
from jax.sharding import Mesh
from jax.sharding import PartitionSpec as P

BLOCK = 114688
PARAM = ("z", "x")
TASK = ("y", "core")
PARAM_TASK = ("z", "x", "y", "core")
LANES = 128
EPSILON = 1e-06

VMEM = pl.BlockSpec(memory_space=pltpu.VMEM)
HBM = pl.BlockSpec(memory_space=pltpu.HBM)
SMEM = pl.BlockSpec(memory_space=pltpu.SMEM)


def copy_for_each(x, axis):
    copies = jnp.broadcast_to(x, (lax.axis_size(axis), *x.shape))
    return lax.all_to_all(copies, axis, split_axis=0, concat_axis=0, tiled=True)


def encode_kernel(core_ref, table_hbm, enc_in_hbm, enc_out_hbm, out_ref, table_ref, enc_in_ref, enc_out_ref, sems):
    copies, rows, _ = out_ref.shape
    start = pl.multiple_of(core_ref[0] * rows, rows)
    loads = [
        pltpu.make_async_copy(table_hbm.at[pl.ds(start, rows), :], table_ref, sems.at[0]),
        pltpu.make_async_copy(enc_in_hbm, enc_in_ref, sems.at[1]),
        pltpu.make_async_copy(enc_out_hbm, enc_out_ref, sems.at[2]),
    ]
    for load in loads:
        load.start()
    loads[0].wait()
    loads[1].wait()
    raw = table_ref[...]
    inner = jax.nn.gelu(jnp.dot(raw, enc_in_ref[...], preferred_element_type=jnp.float32)).astype(jnp.bfloat16)
    loads[2].wait()
    mixed = raw.astype(jnp.float32) + jnp.dot(inner, enc_out_ref[...], preferred_element_type=jnp.float32)
    encoded = mixed.astype(jnp.bfloat16)
    for copy in range(copies):
        out_ref[copy] = encoded


def encode_half(core, task_table, enc_in, enc_out, copies):
    rows, width = task_table.shape[0] // 2, task_table.shape[1]
    return pl.pallas_call(
        encode_kernel,
        out_shape=jax.ShapeDtypeStruct((copies, rows, width), jnp.bfloat16),
        in_specs=[SMEM, HBM, HBM, HBM],
        out_specs=VMEM,
        scratch_shapes=[
            pltpu.VMEM((rows, width), jnp.bfloat16),
            pltpu.VMEM(enc_in.shape, jnp.bfloat16),
            pltpu.VMEM(enc_out.shape, jnp.bfloat16),
            pltpu.SemaphoreType.DMA((3,)),
        ],
        compiler_params=pltpu.CompilerParams(vmem_limit_bytes=8 << 20),
        name="encode_half",
    )(core, task_table, enc_in, enc_out)


def squares_kernel(
    core_ref, ids_ref, mine_ref, other_ref, weights_hbm, embedded_ref, squares_ref, weights_ref, sem, *, shard
):
    load = pltpu.make_async_copy(weights_hbm, weights_ref, sem)
    load.start()
    chunks, groups, lanes = squares_ref.shape
    rows = mine_ref.shape[0]
    half = shard // 2
    columns = weights_ref.shape[0] // groups
    core = core_ref[0]
    ids = jnp.transpose(ids_ref[...])
    place = lax.broadcasted_iota(jnp.int32, (1, rows), 1)
    base = (place // half) * shard + place % half

    def picked(part_ref, which):
        labels = base + which * half
        hot = [(ids[:, k : k + 1] == labels).astype(jnp.bfloat16) for k in range(chunks)]
        return jnp.dot(jnp.concatenate(hot, axis=0), part_ref[...], preferred_element_type=jnp.float32)

    embedded = (picked(mine_ref, core) + picked(other_ref, 1 - core)).astype(jnp.bfloat16)
    embedded_ref[...] = embedded
    load.wait()
    for g in range(groups):
        made = lax.dot_general(
            weights_ref[g * columns : (g + 1) * columns, :],
            embedded,
            (((1,), (1,)), ((), ())),
            preferred_element_type=jnp.float32,
        )
        total = jnp.sum(made * made, axis=0, keepdims=True)
        for k in range(chunks):
            squares_ref[k, g : g + 1, :] = total[:, k * lanes : (k + 1) * lanes]


def squares_of(core, ids, mine, other, weights, groups, shard):
    chunks, lanes = ids.shape
    return pl.pallas_call(
        lambda *refs: squares_kernel(*refs, shard=shard),
        out_shape=(
            jax.ShapeDtypeStruct((chunks * lanes, mine.shape[1]), jnp.bfloat16),
            jax.ShapeDtypeStruct((chunks, groups, lanes), jnp.float32),
        ),
        in_specs=[SMEM, VMEM, VMEM, VMEM, HBM],
        out_specs=(VMEM, VMEM),
        scratch_shapes=[pltpu.VMEM(weights.shape, weights.dtype), pltpu.SemaphoreType.DMA],
        compiler_params=pltpu.CompilerParams(vmem_limit_bytes=24 << 20),
        name="squares",
    )(core, ids, mine, other, weights)


def scale_kernel(weights_ref, embedded_ref, totals_ref, gain_ref, out_ref):
    g = pl.program_id(0)
    chunks = totals_ref.shape[0]
    power = jnp.concatenate([totals_ref[k, pl.ds(g, 1), :] for k in range(chunks)], axis=1)
    inverse = lax.rsqrt(power / BLOCK + EPSILON)
    made = lax.dot_general(
        weights_ref[...], embedded_ref[...], (((1,), (1,)), ((), ())), preferred_element_type=jnp.float32
    )
    out_ref[...] = (made * inverse * gain_ref[...].astype(jnp.float32)).astype(jnp.bfloat16)


def scaled_adapters(weights, embedded, totals, gain):
    chunks, groups, lanes = totals.shape
    columns = weights.shape[0] // groups
    tasks, width = embedded.shape
    return pl.pallas_call(
        scale_kernel,
        grid=(groups,),
        out_shape=jax.ShapeDtypeStruct((groups * columns, tasks), jnp.bfloat16),
        in_specs=[
            pl.BlockSpec((columns, width), lambda g: (g, 0)),
            pl.BlockSpec((tasks, width), lambda g: (0, 0)),
            pl.BlockSpec((chunks, groups, lanes), lambda g: (0, 0, 0)),
            pl.BlockSpec((columns, 1), lambda g: (g, 0)),
        ],
        out_specs=pl.BlockSpec((columns, tasks), lambda g: (g, 0)),
        compiler_params=pltpu.CompilerParams(vmem_limit_bytes=24 << 20),
        name="scale",
    )(weights, embedded, totals, gain)


def on_device(task_ids, task_table, enc_in, enc_out, generator, gain):
    width, groups, columns = generator.shape
    shard = task_table.shape[0]
    core = lax.axis_index("core").reshape(1).astype(jnp.int32)
    weights = generator.transpose(1, 2, 0).reshape(groups * columns, width)
    copies = encode_half(core, task_table, enc_in, enc_out, lax.axis_size(PARAM))
    mine = lax.all_to_all(copies, PARAM, split_axis=0, concat_axis=0, tiled=True).reshape(-1, width)
    ids = copy_for_each(task_ids, TASK)
    mine, ids = lax.optimization_barrier((mine, ids))
    other = lax.ppermute(mine, "core", [(0, 1), (1, 0)])
    embedded, squares = squares_of(core, ids, mine, other, weights, groups, shard)
    spread = lax.all_to_all(squares, TASK, split_axis=0, concat_axis=0, tiled=True)
    totals = copy_for_each(spread.sum(axis=0), PARAM).sum(axis=0)
    totals = copy_for_each(totals, TASK)
    gain_column = gain.reshape(groups * columns, 1)
    made = scaled_adapters(weights, embedded, totals, gain_column)
    return made.reshape(groups, columns, -1).transpose(2, 0, 1)


def solution(mesh):
    torus = Mesh(mesh.devices.reshape(8, 4, 4, 2), PARAM_TASK)
    return jax.shard_map(
        on_device,
        mesh=torus,
        in_specs=(
            P(TASK),
            P(PARAM, None),
            P(),
            P(),
            P(None, None, PARAM_TASK),
            P(None, PARAM_TASK),
        ),
        out_specs=P(None, None, PARAM_TASK),
        check_vma=False,
    )
```

time: 106 us -> 88.9 us (0.84)
  waiting for transfers between devices: 26.9 us -> 5.07 us
  Pallas kernels: 0 us -> 12.2 us
  matrix products: 11.9 us -> 0 us
  other arithmetic: 10.1 us -> 0.05 us
  blocking collectives: 38.5 us -> 48.1 us
  local copies, waits for them, and re-layouts: 2.84 us -> 8.74 us
  starting transfers between devices: 15.3 us -> 14.2 us
    all_to_all x0 -> x2, blocking collectives: none -> 34.7 us  [the longest x1 26.6 us: on_device(): lax.all_to_all(copies, PARAM, split_axis=0, concat_axis=0, tiled=True)]
    all_to_all x2, waiting for transfers between devices: 26.9 us -> 3.53 us  [copy_for_each(): return lax.all_to_all(copies, axis, split_axis=0, concat_axis=0, tiled=True)]
    all_to_all x1, blocking collectives: 26.9 us -> 13.5 us  [copy_for_each(): return lax.all_to_all(copies, axis, split_axis=0, concat_axis=0, tiled=True)]
    pallas_call x0 -> x3, Pallas kernels: none -> 12.2 us  [the longest x1 5.92 us: scaled_adapters(): pl.pallas_call(scale_kernel, grid=(groups,), out_shape=jax.ShapeDtypeStru...]
    dot_general x3 -> x0, matrix products: 11.9 us -> none  [the longest x1 7.32 us: on_device(): jnp.dot(embedded, flat_weights, preferred_element_type=jnp.float32)]
    all_gather x1 -> x0, blocking collectives: 11.6 us -> none  [on_device(): every_id = lax.all_gather(task_ids, TASK, axis=0, tiled=True)]
    convert_element_type x2 -> x0, other arithmetic: 10 us -> none  [the longest x1 10 us: on_device(): return scaled.astype(jnp.bfloat16)]
    unnamed x10, local copies, waits for them, and re-layouts: 0.02 us -> 4.16 us
  transfers between devices with their start and end apart: 2 -> 3, of which waited for: 2 -> 3; matrix products, arithmetic and copies ran while one was open for 0% -> 3% of each run, Pallas kernels for 0% -> 1%
where the time goes in v1:
time: 88.9 us; the launch traced here: 88.4 us
  blocking collectives  48.1 us (54%)
  starting transfers between devices  14.2 us (16%)
  Pallas kernels  12.2 us (14%)
  local copies, waits for them, and re-layouts  8.74 us (10%)
  waiting for transfers between devices  5.07 us (6%)
    all_to_all x1, blocking collectives, on_device(): lax.all_to_all(copies, PARAM, split_axis=0, concat_axis=0, tiled=True)  26.6 us
    all_to_all x1, blocking collectives, copy_for_each(): return lax.all_to_all(copies, axis, split_axis=0, concat_axis=0, tiled=True)  13.5 us
    all_to_all x2, starting transfers between devices, copy_for_each(): return lax.all_to_all(copies, axis, split_axis=0, concat_axis=0, tiled=True)  11.8 us
    all_to_all x1, blocking collectives, on_device(): lax.all_to_all(squares, TASK, split_axis=0, concat_axis=0, tiled=True)  8.03 us
    pallas_call x1, Pallas kernels, scaled_adapters(): pl.pallas_call(scale_kernel, grid=(groups,), out_shape=jax.ShapeDtypeStru...  5.92 us
    pallas_call x1, Pallas kernels, squares_of(): pl.pallas_call(lambda *refs: squares_kernel(*refs, shard=shard), out_shap...  5.72 us
    unnamed x10, local copies, waits for them, and re-layouts  4.16 us
    all_to_all x2, waiting for transfers between devices, copy_for_each(): return lax.all_to_all(copies, axis, split_axis=0, concat_axis=0, tiled=True)  3.53 us
  transfers between devices with their start and end apart: 3, of which 3 were waited for; matrix products, arithmetic and copies ran while one was open for 3% of the time, Pallas kernels for 1%

profile of v1, /device:TPU:1, one launch (start us, length us, event | category | flops | bytes accessed | tf_op | source)
XLA Modules:
  0.0 88.4 jit_solution(7756707963131349611)
XLA Ops:
  0.0 0.0 copy-start.1
  0.0 1.4 %broadcast_in_dim.9 = s32[8,1,128]{2,1,0:T(1,128)} broadcast(s32[128]{0:T(128)} %param.6), dimensions={2} | broadcast | bytes 4608 | tf_op jit(solution)/shard_map/broadcast_in_dim | solution.py:22
  1.4 6.4 %all-to-all-start.1 = ((s32[8,1,128]{2,1,0:T(1,128)}), s32[8,1,128]{2,1,0:T(1,128)S(1)}, u32[]{:S(2)}, u32[]{:S(2)}) async-start(s32[8,1,128]{2,1,0:T(1,128)} %broadcast_in_dim.9), calls=%async_computation.1 | async-start | bytes 8192 | tf_op jit(solution)/shard_map/all_to_all | solution.py:23
  7.8 0.0 copy-start.2
  7.8 0.9 %copy-done.2 = bf16[256,512]{1,0:T(8,128)(2,1)S(1)} copy-done((bf16[256,512]{1,0:T(8,128)(2,1)S(1)}, bf16[256,512]{1,0:T(8,128)(2,1)}, u32[]{:S(2)}) %copy-start.2) | copy-done | bytes 262168
  8.7 0.0 copy-start.3
  8.8 0.9 %copy-done.3 = bf16[512,256]{1,0:T(8,128)(2,1)S(1)} copy-done((bf16[512,256]{1,0:T(8,128)(2,1)S(1)}, bf16[512,256]{1,0:T(8,128)(2,1)}, u32[]{:S(2)}) %copy-start.3) | copy-done | bytes 262168
  9.7 0.0 copy-start.4
  9.7 0.8 copy-done.4
  10.5 0.5 encode_half.1
  11.0 1.4 %all-to-all-done.1 = s32[8,1,128]{2,1,0:T(1,128)S(1)} async-done(((s32[8,1,128]{2,1,0:T(1,128)}), s32[8,1,128]{2,1,0:T(1,128)S(1)}, u32[]{:S(2)}, u32[]{:S(2)}) %all-to-all-start.1) | async-done | bytes 4128 | tf_op jit(solution)/shard_map/all_to_all | solution.py:23
  12.3 26.6 %all_to_all.29 = bf16[32,32,256]{2,1,0:T(8,128)(2,1)S(1)} all-to-all(bf16[32,32,256]{2,1,0:T(8,128)(2,1)S(1)} %encode_half.1), channel_id=1, replica_groups=mesh['z'=8,'x'=4,'y'=4,'core'=2] {'z','x'}, dimensions={0} | all-to-all | bytes 1048576 | tf_op jit(solution)/shard_map/all_to_all | solution.py:152
  39.0 2.4 %collective-permute-start = (bf16[1024,256]{1,0:T(8,128)(2,1)S(1)}, bf16[1024,256]{1,0:T(8,128)(2,1)S(1)}, u32[]{:S(2)}, u32[]{:S(2)}) collective-permute-start(bf16[1024,256]{1,0:T(8,128)(2,1)S(1)} %bitcast.11), channel_id=1, source_target_pairs={{0,1},{1,0},{2,3},{3,2},{4,5},{5,4},{6,7},{7,6},{8,9},{9,8},{10,11... | collective-permute-start | bytes 1572872 | tf_op jit(solution)/shard_map/ppermute | solution.py:155
  41.4 1.5 %collective-permute-done.refs_3_ = bf16[1024,256]{1,0:T(8,128)(2,1)S(1)} collective-permute-done((bf16[1024,256]{1,0:T(8,128)(2,1)S(1)}, bf16[1024,256]{1,0:T(8,128)(2,1)S(1)}, u32[]{:S(2)}, u32[]{:S(2)}) %collective-permute-start) | collective-permute-done | bytes 524320 | tf_op jit(solution)/shard_map/ppermute | solution.py:155
  42.9 0.0 copy-start
  42.9 1.5 %copy-done = bf16[256,8,448]{0,2,1:T(8,128)(2,1)S(1)} copy-done((bf16[256,8,448]{0,2,1:T(8,128)(2,1)S(1)}, bf16[256,8,448]{0,2,1:T(8,128)(2,1)}, u32[]{:S(2)}) %copy-start) | copy-done | bytes 1835032
  44.4 5.7 %squares.1 = (bf16[1024,256]{1,0:T(8,128)(2,1)S(1)}, f32[8,8,128]{2,1,0:T(8,128)S(1)}) custom-call(s32[1]{0:T(128)} %bitcast.2.core_ref.refs_0_, s32[8,128]{1,0:T(8,128)S(1)} %bitcast.13, bf16[1024,256]{1,0:T(8,128)(2,1)S(1)} %bitcast.12, bf16[1024,256]{1,0:T(8,128)(2,1)S(1)} %collective-permute-done.refs_3_, bf16[3584,256]{1,0:T(8,128)(2,1)S(1)} %bitcast.9), custom_call_target="tpu_custom_call" | custom-call | tf_op jit(solution)/shard_map/squares/pallas_call | solution.py:101
  50.2 8.0 %all_to_all.30 = f32[8,8,128]{2,1,0:T(8,128)S(1)} all-to-all(f32[8,8,128]{2,1,0:T(8,128)S(1)} %get-tuple-element.12), channel_id=1, replica_groups=mesh['z'=8,'x'=4,'y'=4,'core'=2] {'y','core'}, dimensions={0} | all-to-all | bytes 65536 | tf_op jit(solution)/shard_map/all_to_all | solution.py:157
  58.2 13.5 %all_to_all.31 = f32[32,8,128]{2,1,0:T(8,128)S(1)} all-to-all(f32[32,8,128]{2,1,0:T(8,128)S(1)} %broadcast_in_dim.10), channel_id=1, replica_groups=mesh['z'=8,'x'=4,'y'=4,'core'=2] {'z','x'}, dimensions={0} | all-to-all | bytes 262144 | tf_op jit(solution)/shard_map/all_to_all | solution.py:23
  71.7 0.6 broadcast_in_dim.11
  72.3 5.4 %all-to-all-start.4 = ((f32[8,8,128]{2,1,0:T(8,128)}), f32[8,8,128]{2,1,0:T(8,128)S(1)}, u32[]{:S(2)}, u32[]{:S(2)}) async-start(f32[8,8,128]{2,1,0:T(8,128)} %broadcast_in_dim.11), calls=%async_computation.4 | async-start | bytes 65536 | tf_op jit(solution)/shard_map/all_to_all | solution.py:23
  77.7 2.6 %reshape.24.gain_ref = bf16[3584,1]{1,0:T(8,128)(2,1)S(1)} reshape(bf16[8,448]{1,0:T(8,128)(2,1)} %param.11) | data formatting | bytes 14336 | tf_op jit(solution)/shard_map/reshape | solution.py:160
  80.3 2.2 %all-to-all-done.4.totals_ref = f32[8,8,128]{2,1,0:T(8,128)S(1)} async-done(((f32[8,8,128]{2,1,0:T(8,128)}), f32[8,8,128]{2,1,0:T(8,128)S(1)}, u32[]{:S(2)}, u32[]{:S(2)}) %all-to-all-start.4) | async-done | bytes 32800 | tf_op jit(solution)/shard_map/all_to_all | solution.py:23
  82.5 0.0 copy-done.1
  82.5 5.9 %scale.1 = bf16[3584,1024]{1,0:T(8,128)(2,1)} custom-call(bf16[3584,256]{1,0:T(8,128)(2,1)S(1)} %bitcast.10, bf16[1024,256]{1,0:T(8,128)(2,1)S(1)} %get-tuple-element.11.embedded_ref, f32[8,8,128]{2,1,0:T(8,128)S(1)} %all-to-all-done.4.totals_ref, bf16[3584,1]{1,0:T(8,128)(2,1)S(1)} %reshape.24.gain_ref), custom_call_target="tpu_custom_call" | custom-call | tf_op jit(solution)/shard_map/scale/pallas_call | solution.py:130
  (3 shorter events, 0.1 us)
Async XLA Ops:
  0.0 82.5 %copy-start.1 = (bf16[256,8,448]{0,2,1:T(8,128)(2,1)S(1)}, bf16[256,8,448]{0,2,1:T(8,128)(2,1)}, u32[]{:S(2)}) copy-start(bf16[256,8,448]{0,2,1:T(8,128)(2,1)} %param.10) | copy-start | bytes 5505028
  1.4 11.0 %all-to-all-start.1 = ((s32[8,1,128]{2,1,0:T(1,128)}), s32[8,1,128]{2,1,0:T(1,128)S(1)}, u32[]{:S(2)}, u32[]{:S(2)}) async-start(s32[8,1,128]{2,1,0:T(1,128)} %broadcast_in_dim.9), calls=%async_computation.1 | async-start | bytes 8192 | tf_op jit(solution)/shard_map/all_to_all | solution.py:23
  7.8 0.9 %copy-start.2 = (bf16[256,512]{1,0:T(8,128)(2,1)S(1)}, bf16[256,512]{1,0:T(8,128)(2,1)}, u32[]{:S(2)}) copy-start(bf16[256,512]{1,0:T(8,128)(2,1)} %enc_in_hbm.1) | copy-start | bytes 786436
  8.7 0.9 %copy-start.3 = (bf16[512,256]{1,0:T(8,128)(2,1)S(1)}, bf16[512,256]{1,0:T(8,128)(2,1)}, u32[]{:S(2)}) copy-start(bf16[512,256]{1,0:T(8,128)(2,1)} %enc_out_hbm.1) | copy-start | bytes 786436
  9.7 0.8 copy-start.4
  39.0 3.9 %collective-permute-start = (bf16[1024,256]{1,0:T(8,128)(2,1)S(1)}, bf16[1024,256]{1,0:T(8,128)(2,1)S(1)}, u32[]{:S(2)}, u32[]{:S(2)}) collective-permute-start(bf16[1024,256]{1,0:T(8,128)(2,1)S(1)} %bitcast.11), channel_id=1, source_target_pairs={{0,1},{1,0},{2,3},{3,2},{4,5},{5,4},{6,7},{7,6},{8,9},{9,8},{10,11... | collective-permute-start | bytes 1572872 | tf_op jit(solution)/shard_map/ppermute | solution.py:155
  42.9 1.5 %copy-start = (bf16[256,8,448]{0,2,1:T(8,128)(2,1)S(1)}, bf16[256,8,448]{0,2,1:T(8,128)(2,1)}, u32[]{:S(2)}) copy-start(bf16[256,8,448]{0,2,1:T(8,128)(2,1)} %param.10) | copy-start | bytes 5505028
  72.3 10.1 %all-to-all-start.4 = ((f32[8,8,128]{2,1,0:T(8,128)}), f32[8,8,128]{2,1,0:T(8,128)S(1)}, u32[]{:S(2)}, u32[]{:S(2)}) async-start(f32[8,8,128]{2,1,0:T(8,128)} %broadcast_in_dim.11), calls=%async_computation.4 | async-start | bytes 65536 | tf_op jit(solution)/shard_map/all_to_all | solution.py:23

commit v2 on v1

v2 whole, which is shorter than its diff:
```python
import jax
import jax.numpy as jnp
from jax import lax
from jax.experimental import pallas as pl
from jax.experimental.pallas import tpu as pltpu
from jax.sharding import Mesh
from jax.sharding import PartitionSpec as P

BLOCK = 114688
PARAM = ("z", "x")
TASK = ("y", "core")
PARAM_TASK = ("z", "x", "y", "core")
LANES = 128
EPSILON = 1e-06

VMEM = pl.BlockSpec(memory_space=pltpu.VMEM)
HBM = pl.BlockSpec(memory_space=pltpu.HBM)
SMEM = pl.BlockSpec(memory_space=pltpu.SMEM)
ROWS_BY_ROWS = (((1,), (1,)), ((), ()))


def in_hbm(x):
    return pltpu.with_memory_space_constraint(x, pltpu.HBM)


def limit(mebibytes):
    return pltpu.CompilerParams(vmem_limit_bytes=mebibytes << 20)


def exchange(x, axis):
    return lax.all_to_all(x, axis, split_axis=0, concat_axis=0, tiled=True)


def copy_for_each(x, axis):
    return exchange(jnp.broadcast_to(x, (lax.axis_size(axis), *x.shape)), axis)


def encode_kernel(core_ref, table_hbm, enc_in_hbm, enc_out_hbm, out_ref, table_ref, enc_in_ref, enc_out_ref, sems):
    copies, rows, _ = out_ref.shape
    start = pl.multiple_of(core_ref[0] * rows, rows)
    loads = [
        pltpu.make_async_copy(table_hbm.at[pl.ds(start, rows), :], table_ref, sems.at[0]),
        pltpu.make_async_copy(enc_in_hbm, enc_in_ref, sems.at[1]),
        pltpu.make_async_copy(enc_out_hbm, enc_out_ref, sems.at[2]),
    ]
    for load in loads:
        load.start()
    loads[0].wait()
    loads[1].wait()
    raw = table_ref[...]
    inner = jax.nn.gelu(jnp.dot(raw, enc_in_ref[...], preferred_element_type=jnp.float32)).astype(jnp.bfloat16)
    loads[2].wait()
    mixed = raw.astype(jnp.float32) + jnp.dot(inner, enc_out_ref[...], preferred_element_type=jnp.float32)
    encoded = mixed.astype(jnp.bfloat16)
    for copy in range(copies):
        out_ref[copy] = encoded


def encode_half(core, task_table, enc_in, enc_out, copies):
    rows, width = task_table.shape[0] // 2, task_table.shape[1]
    return pl.pallas_call(
        encode_kernel,
        out_shape=jax.ShapeDtypeStruct((copies, rows, width), jnp.bfloat16),
        in_specs=[SMEM, HBM, HBM, HBM],
        out_specs=VMEM,
        scratch_shapes=[
            pltpu.VMEM((rows, width), jnp.bfloat16),
            pltpu.VMEM(enc_in.shape, jnp.bfloat16),
            pltpu.VMEM(enc_out.shape, jnp.bfloat16),
            pltpu.SemaphoreType.DMA((3,)),
        ],
        compiler_params=limit(8),
        name="encode_half",
    )(core, in_hbm(task_table), in_hbm(enc_in), in_hbm(enc_out))


def picked_rows(ids_ref, part_ref, which, half):
    chunks = ids_ref.shape[0]
    ids = jnp.transpose(ids_ref[...])
    place = lax.broadcasted_iota(jnp.int32, (1, part_ref.shape[0]), 1)
    labels = (place // half) * (2 * half) + place % half + which * half
    hot = [(ids[:, k : k + 1] == labels).astype(jnp.bfloat16) for k in range(chunks)]
    return jnp.dot(jnp.concatenate(hot, axis=0), part_ref[...], preferred_element_type=jnp.float32)


def first_half(core, ids, mine, weights, half):
    def kernel(core_ref, ids_ref, mine_ref, weights_hbm, part_ref, weights_ref, sem):
        load = pltpu.make_async_copy(weights_hbm, weights_ref, sem)
        load.start()
        part_ref[...] = picked_rows(ids_ref, mine_ref, core_ref[0], half).astype(jnp.bfloat16)
        load.wait()

    return pl.pallas_call(
        kernel,
        out_shape=(
            jax.ShapeDtypeStruct((ids.size, mine.shape[1]), jnp.bfloat16),
            jax.ShapeDtypeStruct(weights.shape, weights.dtype),
        ),
        in_specs=[SMEM, VMEM, VMEM, HBM],
        out_specs=(VMEM, VMEM),
        scratch_shapes=[pltpu.SemaphoreType.DMA],
        compiler_params=limit(16),
        name="first_half",
    )(core, ids, mine, in_hbm(weights))


def squares_of(core, ids, part, other, weights, groups, half):
    chunks, lanes = ids.shape
    columns = weights.shape[0] // groups

    def kernel(core_ref, ids_ref, part_ref, other_ref, weights_ref, embedded_ref, squares_ref):
        rest = picked_rows(ids_ref, other_ref, 1 - core_ref[0], half)
        embedded = (part_ref[...].astype(jnp.float32) + rest).astype(jnp.bfloat16)
        embedded_ref[...] = embedded
        for g in range(groups):
            made = lax.dot_general(
                weights_ref[g * columns : (g + 1) * columns, :],
                embedded,
                ROWS_BY_ROWS,
                preferred_element_type=jnp.float32,
            )
            total = jnp.sum(made * made, axis=0, keepdims=True)
            for k in range(chunks):
                squares_ref[k, g : g + 1, :] = total[:, k * lanes : (k + 1) * lanes]

    return pl.pallas_call(
        kernel,
        out_shape=(
            jax.ShapeDtypeStruct(part.shape, jnp.bfloat16),
            jax.ShapeDtypeStruct((chunks, groups, lanes), jnp.float32),
        ),
        in_specs=[SMEM, VMEM, VMEM, VMEM, VMEM],
        out_specs=(VMEM, VMEM),
        compiler_params=limit(24),
        name="squares",
    )(core, ids, part, other, weights)


def scaled_adapters(weights, embedded, totals, gain):
    chunks, groups, lanes = totals.shape
    columns = weights.shape[0] // groups
    tasks, width = embedded.shape
    padding = -columns % LANES

    def kernel(weights_ref, embedded_ref, totals_ref, gain_ref, out_hbm, out_ref, sems):
        gains = gain_ref[...].astype(jnp.float32)
        gains = jnp.transpose(jnp.concatenate([gains, jnp.zeros((groups, padding), jnp.float32)], axis=1))
        stores = []
        for g in range(groups):
            rows = pl.ds(g * columns, columns)
            power = jnp.concatenate([totals_ref[k, g : g + 1, :] for k in range(chunks)], axis=1)
            inverse = lax.rsqrt(power / BLOCK + EPSILON)
            made = lax.dot_general(
                weights_ref[g * columns : (g + 1) * columns, :],
                embedded_ref[...],
                ROWS_BY_ROWS,
                preferred_element_type=jnp.float32,
            )
            out_ref[g] = (made * inverse * gains[:columns, g : g + 1]).astype(jnp.bfloat16)
            store = pltpu.make_async_copy(out_ref.at[g], out_hbm.at[rows, :], sems.at[g])
            store.start()
            stores.append(store)
        for store in stores:
            store.wait()

    return pl.pallas_call(
        kernel,
        out_shape=jax.ShapeDtypeStruct((groups * columns, tasks), jnp.bfloat16),
        in_specs=[VMEM, VMEM, VMEM, VMEM],
        out_specs=HBM,
        scratch_shapes=[pltpu.VMEM((groups, columns, tasks), jnp.bfloat16), pltpu.SemaphoreType.DMA((groups,))],
        compiler_params=limit(24),
        name="scale",
    )(weights, embedded, totals, gain)


def on_device(task_ids, task_table, enc_in, enc_out, generator, gain):
    width, groups, columns = generator.shape
    half = task_table.shape[0] // 2
    core = lax.axis_index("core").reshape(1).astype(jnp.int32)
    weights = generator.transpose(1, 2, 0).reshape(groups * columns, width)
    copies = encode_half(core, task_table, enc_in, enc_out, lax.axis_size(PARAM))
    task_ids, copies = lax.optimization_barrier((task_ids, copies))
    mine = exchange(copies, PARAM).reshape(-1, width)
    ids = lax.all_gather(task_ids.reshape(1, -1), TASK, axis=0, tiled=True)
    mine, ids = lax.optimization_barrier((mine, ids))
    other = lax.ppermute(mine, "core", [(0, 1), (1, 0)])
    part, weights = first_half(core, ids, mine, weights, half)
    embedded, squares = squares_of(core, ids, part, other, weights, groups, half)
    totals = copy_for_each(exchange(squares, TASK).sum(axis=0), PARAM).sum(axis=0)
    totals = copy_for_each(totals, TASK)
    made = scaled_adapters(weights, embedded, totals, gain)
    return made.reshape(groups, columns, -1).transpose(2, 0, 1)


def solution(mesh):
    torus = Mesh(mesh.devices.reshape(8, 4, 4, 2), PARAM_TASK)
    return jax.shard_map(
        on_device,
        mesh=torus,
        in_specs=(
            P(TASK),
            P(PARAM, None),
            P(),
            P(),
            P(None, None, PARAM_TASK),
            P(None, PARAM_TASK),
        ),
        out_specs=P(None, None, PARAM_TASK),
        check_vma=False,
    )
```

time: 88.9 us -> 74 us (0.83)
  local copies, waits for them, and re-layouts: 8.74 us -> 0.03 us
  blocking collectives: 48.1 us -> 43.7 us
  Pallas kernels: 12.2 us -> 10.9 us
    all_to_all x3, blocking collectives: 48.1 us -> 32.1 us  [exchange(): return lax.all_to_all(x, axis, split_axis=0, concat_axis=0, tiled=True)]
    all_gather x0 -> x1, blocking collectives: none -> 11.6 us  [on_device(): ids = lax.all_gather(task_ids.reshape(1, -1), TASK, axis=0, tiled=True)]
    unnamed x10 -> x4, local copies, waits for them, and re-layouts: 4.16 us -> 0.01 us
    pallas_call x2 -> x3, Pallas kernels: 11.6 us -> 8.67 us  [the longest x1 3.6 us: squares_of(): pl.pallas_call(kernel, out_shape=(jax.ShapeDtypeStruct(part.shape, jnp.bf...]
    reshape x1 -> x0, local copies, waits for them, and re-layouts: 2.56 us -> none  [on_device(): gain_column = gain.reshape(groups * columns, 1)]
    broadcast_in_dim x3 -> x2, local copies, waits for them, and re-layouts: 2.02 us -> 0.02 us  [copy_for_each(): return exchange(jnp.broadcast_to(x, (lax.axis_size(axis), *x.shape)), axis)]
    pallas_call x1, Pallas kernels: 0.52 us -> 2.24 us  [encode_half(): pl.pallas_call(encode_kernel, out_shape=jax.ShapeDtypeStruct((copies, row...]
    ppermute x1, waiting for transfers between devices: 1.54 us -> 0.01 us  [on_device(): other = lax.ppermute(mine, 'core', [(0, 1), (1, 0)])]
  transfers between devices with their start and end apart: 3 -> 2, of which waited for: 3 -> 1; matrix products, arithmetic and copies ran while one was open for 3% -> 0% of each run, Pallas kernels for 1% -> 2%
where the time goes in v2:
time: 74 us; the launch traced here: 73.7 us
  blocking collectives  43.7 us (59%)
  starting transfers between devices  14.3 us (19%)
  Pallas kernels  10.9 us (15%)
  waiting for transfers between devices  4.68 us (6%)
    all_to_all x3, blocking collectives, exchange(): return lax.all_to_all(x, axis, split_axis=0, concat_axis=0, tiled=True)  32.1 us
    all_to_all x1, starting transfers between devices, exchange(): return lax.all_to_all(x, axis, split_axis=0, concat_axis=0, tiled=True)  11.9 us
    all_gather x1, blocking collectives, on_device(): ids = lax.all_gather(task_ids.reshape(1, -1), TASK, axis=0, tiled=True)  11.6 us
    all_to_all x1, waiting for transfers between devices, exchange(): return lax.all_to_all(x, axis, split_axis=0, concat_axis=0, tiled=True)  4.68 us
    pallas_call x1, Pallas kernels, squares_of(): pl.pallas_call(kernel, out_shape=(jax.ShapeDtypeStruct(part.shape, jnp.bf...  3.6 us
    pallas_call x1, Pallas kernels, scaled_adapters(): pl.pallas_call(kernel, out_shape=jax.ShapeDtypeStruct((groups * columns,...  3.55 us
    ppermute x1, starting transfers between devices, on_device(): other = lax.ppermute(mine, 'core', [(0, 1), (1, 0)])  2.43 us
    pallas_call x1, Pallas kernels, encode_half(): pl.pallas_call(encode_kernel, out_shape=jax.ShapeDtypeStruct((copies, row...  2.24 us
  transfers between devices with their start and end apart: 2, of which 1 were waited for; matrix products, arithmetic and copies ran while one was open for 0% of the time, Pallas kernels for 2%

profile of v2, /device:TPU:1, one launch (start us, length us, event | category | flops | bytes accessed | tf_op | source)
XLA Modules:
  0.0 73.7 jit_solution(7422348528218117417)
XLA Ops:
  0.0 0.0 copy-start.1
  0.0 2.2 %encode_half.1 = bf16[32,32,256]{2,1,0:T(8,128)(2,1)} custom-call(s32[1]{0:T(128)} %bitcast.core_ref, bf16[64,256]{1,0:T(8,128)(2,1)} %table_hbm.1, bf16[256,512]{1,0:T(8,128)(2,1)} %enc_in_hbm.1, bf16[512,256]{1,0:T(8,128)(2,1)} %enc_out_hbm.1), custom_call_target="tpu_custom_call" | custom-call | tf_op jit(solution)/shard_map/encode_half/pallas_call | solution.py:61
  2.3 11.9 %all-to-all-start = ((bf16[32,32,256]{2,1,0:T(8,128)(2,1)}), bf16[32,32,256]{2,1,0:T(8,128)(2,1)S(1)}, u32[]{:S(2)}, u32[]{:S(2)}) async-start(bf16[32,32,256]{2,1,0:T(8,128)(2,1)} %encode_half.1), calls=%async_computation | async-start | bytes 1048576 | tf_op jit(solution)/shard_map/all_to_all | solution.py:31
  14.1 0.0 copy-done.1
  14.1 11.6 %all-gather.1 = s32[8,1,128]{2,1,0:T(1,128)S(1)} all-gather(s32[1,1,128]{2,1,0:T(1,128)S(1)} %bitcast.15), channel_id=2, replica_groups=mesh['z'=8,'x'=4,'y'=4,'core'=2] {'y','core'}, dimensions={0}, use_global_device_ids=true | all-gather | bytes 4608 | tf_op jit(solution)/shard_map/all_gather | solution.py:185
  25.7 4.7 %all-to-all-done = bf16[32,32,256]{2,1,0:T(8,128)(2,1)S(1)} async-done(((bf16[32,32,256]{2,1,0:T(8,128)(2,1)}), bf16[32,32,256]{2,1,0:T(8,128)(2,1)S(1)}, u32[]{:S(2)}, u32[]{:S(2)}) %all-to-all-start) | async-done | bytes 524320 | tf_op jit(solution)/shard_map/all_to_all | solution.py:31
  30.4 2.4 %collective-permute-start = (bf16[1024,256]{1,0:T(8,128)(2,1)S(1)}, bf16[1024,256]{1,0:T(8,128)(2,1)S(1)}, u32[]{:S(2)}, u32[]{:S(2)}) collective-permute-start(bf16[1024,256]{1,0:T(8,128)(2,1)S(1)} %bitcast.10), channel_id=1, source_target_pairs={{0,1},{1,0},{2,3},{3,2},{4,5},{5,4},{6,7},{7,6},{8,9},{9,8},{10,11... | collective-permute-start | bytes 1572872 | tf_op jit(solution)/shard_map/ppermute | solution.py:187
  32.8 1.5 %first_half.1 = (bf16[1024,256]{1,0:T(8,128)(2,1)S(1)}, bf16[3584,256]{1,0:T(8,128)(2,1)S(1)}) custom-call(s32[1]{0:T(128)} %bitcast.core_ref, s32[8,128]{1,0:T(8,128)S(1)} %bitcast.12, bf16[1024,256]{1,0:T(8,128)(2,1)S(1)} %bitcast.11, bf16[3584,256]{1,0:T(8,128)(2,1)} %bitcast.14), custom_call_target="tpu_custom_call" | custom-call | tf_op jit(solution)/shard_map/first_half/pallas_call | solution.py:93
  34.4 0.0 copy-start
  34.4 0.0 collective-permute-done.other_ref
  34.4 3.6 %squares.1 = (bf16[1024,256]{1,0:T(8,128)(2,1)S(1)}, f32[8,8,128]{2,1,0:T(8,128)S(1)}) custom-call(s32[1]{0:T(128)} %bitcast.core_ref, s32[8,128]{1,0:T(8,128)S(1)} %bitcast.13, bf16[1024,256]{1,0:T(8,128)(2,1)S(1)} %get-tuple-element.18.part_ref, bf16[1024,256]{1,0:T(8,128)(2,1)S(1)} %collective-permute-done.other_ref, ...), custom_call_target="tpu_custom_call" | custom-call | tf_op jit(solution)/shard_map/squares/pallas_call | solution.py:126
  38.0 9.3 %all_to_all.20 = f32[8,8,128]{2,1,0:T(8,128)S(1)} all-to-all(f32[8,8,128]{2,1,0:T(8,128)S(1)} %get-tuple-element.20), channel_id=1, replica_groups=mesh['z'=8,'x'=4,'y'=4,'core'=2] {'y','core'}, dimensions={0} | all-to-all | bytes 65536 | tf_op jit(solution)/shard_map/all_to_all | solution.py:31
  47.4 13.5 %all_to_all.21 = f32[32,8,128]{2,1,0:T(8,128)S(1)} all-to-all(f32[32,8,128]{2,1,0:T(8,128)S(1)} %broadcast_in_dim.6), channel_id=1, replica_groups=mesh['z'=8,'x'=4,'y'=4,'core'=2] {'z','x'}, dimensions={0} | all-to-all | bytes 262144 | tf_op jit(solution)/shard_map/all_to_all | solution.py:31
  60.9 9.2 %all_to_all.22.totals_ref = f32[8,8,128]{2,1,0:T(8,128)S(1)} all-to-all(f32[8,8,128]{2,1,0:T(8,128)S(1)} %broadcast_in_dim.7), channel_id=1, replica_groups=mesh['z'=8,'x'=4,'y'=4,'core'=2] {'y','core'}, dimensions={0} | all-to-all | bytes 65536 | tf_op jit(solution)/shard_map/all_to_all | solution.py:31
  70.2 0.0 copy-done
  70.2 3.5 %scale.1 = bf16[3584,1024]{1,0:T(8,128)(2,1)} custom-call(bf16[3584,256]{1,0:T(8,128)(2,1)S(1)} %get-tuple-element.17.weights_ref, bf16[1024,256]{1,0:T(8,128)(2,1)S(1)} %get-tuple-element.19.embedded_ref, f32[8,8,128]{2,1,0:T(8,128)S(1)} %all_to_all.22.totals_ref, bf16[8,448]{1,0:T(8,128)(2,1)S(1)} %copy-done), custom_call_target="tpu_custom_call" | custom-call | tf_op jit(solution)/shard_map/scale/pallas_call | solution.py:166
  (4 shorter events, 0.1 us)
Async XLA Ops:
  0.0 14.1 %copy-start.1 = (s32[128]{0:T(128)S(1)}, s32[128]{0:T(128)}, u32[]{:S(2)}) copy-start(s32[128]{0:T(128)} %param.6) | copy-start | bytes 1540
  2.3 28.2 %all-to-all-start = ((bf16[32,32,256]{2,1,0:T(8,128)(2,1)}), bf16[32,32,256]{2,1,0:T(8,128)(2,1)S(1)}, u32[]{:S(2)}, u32[]{:S(2)}) async-start(bf16[32,32,256]{2,1,0:T(8,128)(2,1)} %encode_half.1), calls=%async_computation | async-start | bytes 1048576 | tf_op jit(solution)/shard_map/all_to_all | solution.py:31
  30.4 4.0 %collective-permute-start = (bf16[1024,256]{1,0:T(8,128)(2,1)S(1)}, bf16[1024,256]{1,0:T(8,128)(2,1)S(1)}, u32[]{:S(2)}, u32[]{:S(2)}) collective-permute-start(bf16[1024,256]{1,0:T(8,128)(2,1)S(1)} %bitcast.10), channel_id=1, source_target_pairs={{0,1},{1,0},{2,3},{3,2},{4,5},{5,4},{6,7},{7,6},{8,9},{9,8},{10,11... | collective-permute-start | bytes 1572872 | tf_op jit(solution)/shard_map/ppermute | solution.py:187
  34.4 35.8 %copy-start = (bf16[8,448]{1,0:T(8,128)(2,1)S(1)}, bf16[8,448]{1,0:T(8,128)(2,1)}, u32[]{:S(2)}) copy-start(bf16[8,448]{1,0:T(8,128)(2,1)} %gain_ref.1) | copy-start | bytes 21508

commit v3 on v2

--- a/solution.py
+++ b/solution.py
@@ -104,51 +104,108 @@
     )(core, ids, mine, in_hbm(weights))
 
 
-def squares_of(core, ids, part, other, weights, groups, half):
-    chunks, lanes = ids.shape
+def embed(core, ids, part, other, half):
+    def kernel(core_ref, ids_ref, part_ref, other_ref, embedded_ref):
+        rest = picked_rows(ids_ref, other_ref, 1 - core_ref[0], half)
+        embedded_ref[...] = (part_ref[...].astype(jnp.float32) + rest).astype(jnp.bfloat16)
+
+    return pl.pallas_call(
+        kernel,
+        out_shape=jax.ShapeDtypeStruct(part.shape, jnp.bfloat16),
+        in_specs=[SMEM, VMEM, VMEM, VMEM],
+        out_specs=VMEM,
+        compiler_params=limit(16),
+        name="embed",
+    )(core, ids, part, other)
+
+
+def squares_of(side, embedded, weights, groups):
     columns = weights.shape[0] // groups
-
-    def kernel(core_ref, ids_ref, part_ref, other_ref, weights_ref, embedded_ref, squares_ref):
-        rest = picked_rows(ids_ref, other_ref, 1 - core_ref[0], half)
-        embedded = (part_ref[...].astype(jnp.float32) + rest).astype(jnp.bfloat16)
-        embedded_ref[...] = embedded
+    tasks = embedded.shape[0] // 2
+    chunks = tasks // LANES
+
+    def kernel(side_ref, embedded_ref, weights_ref, squares_ref):
+        wanted = embedded_ref[pl.ds(pl.multiple_of(side_ref[0] * tasks, tasks), tasks), :]
         for g in range(groups):
             made = lax.dot_general(
                 weights_ref[g * columns : (g + 1) * columns, :],
-                embedded,
+                wanted,
                 ROWS_BY_ROWS,
                 preferred_element_type=jnp.float32,
             )
             total = jnp.sum(made * made, axis=0, keepdims=True)
             for k in range(chunks):
-                squares_ref[k, g : g + 1, :] = total[:, k * lanes : (k + 1) * lanes]
-
-    return pl.pallas_call(
-        kernel,
-        out_shape=(
-            jax.ShapeDtypeStruct(part.shape, jnp.bfloat16),
-            jax.ShapeDtypeStruct((chunks, groups, lanes), jnp.float32),
-        ),
-        in_specs=[SMEM, VMEM, VMEM, VMEM, VMEM],
-        out_specs=(VMEM, VMEM),
-        compiler_params=limit(24),
+                squares_ref[k, g : g + 1, :] = total[:, k * LANES : (k + 1) * LANES]
+
+    return pl.pallas_call(
+        kernel,
+        out_shape=jax.ShapeDtypeStruct((chunks, groups, LANES), jnp.float32),
+        in_specs=[SMEM, VMEM, VMEM],
+        out_specs=VMEM,
+        compiler_params=limit(16),
         name="squares",
-    )(core, ids, part, other, weights)
-
-
-def scaled_adapters(weights, embedded, totals, gain):
-    chunks, groups, lanes = totals.shape
-    columns = weights.shape[0] // groups
+    )(side, embedded, weights)
+
+
+def split_by_row(row, keep, received):
+    count = keep.shape[0]
+
+    def kernel(row_ref, keep_ref, received_ref, *out_refs):
+        for ahead, out_ref in enumerate(out_refs):
+            chunk = lax.rem(row_ref[0] + ahead, count)
+            out_ref[...] = keep_ref[chunk] + received_ref[chunk]
+
+    return pl.pallas_call(
+        kernel,
+        out_shape=[jax.ShapeDtypeStruct(keep.shape[1:], jnp.float32)] * count,
+        in_specs=[SMEM, VMEM, VMEM],
+        out_specs=[VMEM] * count,
+        compiler_params=limit(4),
+        name="split_by_row",
+    )(row, keep, received)
+
+
+def sum_for_each(pieces, copies):
+    def kernel(*refs):
+        total = refs[0][...]
+        for piece_ref in refs[1:-1]:
+            total = total + piece_ref[...]
+        for copy in range(copies):
+            refs[-1][copy] = total
+
+    return pl.pallas_call(
+        kernel,
+        out_shape=jax.ShapeDtypeStruct((copies, *pieces[0].shape), jnp.float32),
+        in_specs=[VMEM] * len(pieces),
+        out_specs=VMEM,
+        compiler_params=limit(4),
+        name="sum_for_each",
+    )(*pieces)
+
+
+def around(x, axis, ahead):
+    size = lax.axis_size(axis)
+    return lax.ppermute(x, axis, [(i, (i + ahead) % size) for i in range(size)])
+
+
+def scaled_adapters(core, row, weights, embedded, pairs, gain):
+    rows_of_chips = len(pairs)
+    groups, columns = gain.shape
     tasks, width = embedded.shape
     padding = -columns % LANES
 
-    def kernel(weights_ref, embedded_ref, totals_ref, gain_ref, out_hbm, out_ref, sems):
+    def kernel(core_ref, row_ref, weights_ref, embedded_ref, *refs):
+        pair_refs, (gain_ref, out_hbm, out_ref, totals_ref, sems) = refs[:rows_of_chips], refs[rows_of_chips:]
+        for behind in range(rows_of_chips):
+            chunk = lax.rem(row_ref[0] + rows_of_chips - behind, rows_of_chips)
+            totals_ref[core_ref[0] * rows_of_chips + chunk] = pair_refs[behind][0]
+            totals_ref[(1 - core_ref[0]) * rows_of_chips + chunk] = pair_refs[behind][1]
         gains = gain_ref[...].astype(jnp.float32)
         gains = jnp.transpose(jnp.concatenate([gains, jnp.zeros((groups, padding), jnp.float32)], axis=1))
         stores = []
         for g in range(groups):
             rows = pl.ds(g * columns, columns)
-            power = jnp.concatenate([totals_ref[k, g : g + 1, :] for k in range(chunks)], axis=1)
+            power = jnp.concatenate([totals_ref[k, g : g + 1, :] for k in range(2 * rows_of_chips)], axis=1)
             inverse = lax.rsqrt(power / BLOCK + EPSILON)
             made = lax.dot_general(
                 weights_ref[g * columns : (g + 1) * columns, :],
@@ -166,18 +223,23 @@
     return pl.pallas_call(
         kernel,
         out_shape=jax.ShapeDtypeStruct((groups * columns, tasks), jnp.bfloat16),
-        in_specs=[VMEM, VMEM, VMEM, VMEM],
+        in_specs=[SMEM, SMEM] + [VMEM] * (3 + len(pairs)),
         out_specs=HBM,
-        scratch_shapes=[pltpu.VMEM((groups, columns, tasks), jnp.bfloat16), pltpu.SemaphoreType.DMA((groups,))],
+        scratch_shapes=[
+            pltpu.VMEM((groups, columns, tasks), jnp.bfloat16),
+            pltpu.VMEM((2 * rows_of_chips, groups, LANES), jnp.float32),
+            pltpu.SemaphoreType.DMA((groups,)),
+        ],
         compiler_params=limit(24),
         name="scale",
-    )(weights, embedded, totals, gain)
+    )(core, row, weights, embedded, *pairs, gain)
 
 
 def on_device(task_ids, task_table, enc_in, enc_out, generator, gain):
     width, groups, columns = generator.shape
     half = task_table.shape[0] // 2
     core = lax.axis_index("core").reshape(1).astype(jnp.int32)
+    row = lax.axis_index("y").reshape(1).astype(jnp.int32)
     weights = generator.transpose(1, 2, 0).reshape(groups * columns, width)
     copies = encode_half(core, task_table, enc_in, enc_out, lax.axis_size(PARAM))
     task_ids, copies = lax.optimization_barrier((task_ids, copies))
@@ -186,10 +248,17 @@
     mine, ids = lax.optimization_barrier((mine, ids))
     other = lax.ppermute(mine, "core", [(0, 1), (1, 0)])
     part, weights = first_half(core, ids, mine, weights, half)
-    embedded, squares = squares_of(core, ids, part, other, weights, groups, half)
-    totals = copy_for_each(exchange(squares, TASK).sum(axis=0), PARAM).sum(axis=0)
-    totals = copy_for_each(totals, TASK)
-    made = scaled_adapters(weights, embedded, totals, gain)
+    embedded = embed(core, ids, part, other, half)
+    given = squares_of(1 - core, embedded, weights, groups)
+    received = around(given, "core", 1)
+    kept = squares_of(core, embedded, weights, groups)
+    own, *others = split_by_row(row, kept, received)
+    steps = range(1, len(others) + 1)
+    arrived = [around(piece, "y", ahead) for ahead, piece in zip(steps, others)]
+    totals = exchange(sum_for_each([own, *arrived], lax.axis_size(PARAM)), PARAM).sum(axis=0)
+    pair = jnp.stack([totals, around(totals, "core", 1)])
+    pairs = [pair] + [around(pair, "y", ahead) for ahead in steps]
+    made = scaled_adapters(core, row, weights, embedded, pairs, gain)
     return made.reshape(groups, columns, -1).transpose(2, 0, 1)
 
 

time: 74 us -> 72.4 us (0.978)
  blocking collectives: 43.7 us -> 25.1 us
  starting transfers between devices: 14.3 us -> 26 us
  waiting for transfers between devices: 4.68 us -> 10.4 us
    all_to_all x3 -> x1, blocking collectives: 32.1 us -> 13.5 us  [exchange(): return lax.all_to_all(x, axis, split_axis=0, concat_axis=0, tiled=True)]
    ppermute x0 -> x8, starting transfers between devices: none -> 11.7 us  [around(): return lax.ppermute(x, axis, [(i, (i + ahead) % size) for i in range(size)])]
    ppermute x0 -> x8, waiting for transfers between devices: none -> 5.7 us  [around(): return lax.ppermute(x, axis, [(i, (i + ahead) % size) for i in range(size)])]
    pallas_call x1 -> x5, Pallas kernels: 3.6 us -> 3.18 us  [the longest x2 2.32 us: squares_of(): pl.pallas_call(kernel, out_shape=jax.ShapeDtypeStruct((chunks, groups, LA...]
  transfers between devices with their start and end apart: 2 -> 10, of which waited for: 1 -> 6; matrix products, arithmetic and copies ran while one was open for 0% -> 0% of each run, Pallas kernels for 2% -> 4%
where the time goes in v3:
time: 72.4 us; the launch traced here: 72.1 us
  starting transfers between devices  26 us (36%)
  blocking collectives  25.1 us (35%)
  Pallas kernels  10.5 us (15%)
  waiting for transfers between devices  10.4 us (14%)
    all_to_all x1, blocking collectives, exchange(): return lax.all_to_all(x, axis, split_axis=0, concat_axis=0, tiled=True)  13.5 us
    all_to_all x1, starting transfers between devices, exchange(): return lax.all_to_all(x, axis, split_axis=0, concat_axis=0, tiled=True)  11.9 us
    ppermute x8, starting transfers between devices, around(): return lax.ppermute(x, axis, [(i, (i + ahead) % size) for i in range(size)])  11.7 us
    all_gather x1, blocking collectives, on_device(): ids = lax.all_gather(task_ids.reshape(1, -1), TASK, axis=0, tiled=True)  11.6 us
    ppermute x8, waiting for transfers between devices, around(): return lax.ppermute(x, axis, [(i, (i + ahead) % size) for i in range(size)])  5.7 us
    all_to_all x1, waiting for transfers between devices, exchange(): return lax.all_to_all(x, axis, split_axis=0, concat_axis=0, tiled=True)  4.68 us
    pallas_call x1, Pallas kernels, scaled_adapters(): pl.pallas_call(kernel, out_shape=jax.ShapeDtypeStruct((groups * columns,...  3.55 us
    ppermute x1, starting transfers between devices, on_device(): other = lax.ppermute(mine, 'core', [(0, 1), (1, 0)])  2.43 us
  transfers between devices with their start and end apart: 10, of which 6 were waited for; matrix products, arithmetic and copies ran while one was open for 0% of the time, Pallas kernels for 4%

profile of v3, /device:TPU:1, one launch (start us, length us, event | category | flops | bytes accessed | tf_op | source)
XLA Modules:
  0.0 72.1 jit_solution(14069905995424291333)
XLA Ops:
  0.0 0.0 copy-start.1
  0.0 2.2 %encode_half.1 = bf16[32,32,256]{2,1,0:T(8,128)(2,1)} custom-call(s32[1]{0:T(128)} %bitcast.core_ref.side_ref, bf16[64,256]{1,0:T(8,128)(2,1)} %table_hbm.1, bf16[256,512]{1,0:T(8,128)(2,1)} %enc_in_hbm.1, bf16[512,256]{1,0:T(8,128)(2,1)} %enc_out_hbm.1), custom_call_target="tpu_custom_call" | custom-call | tf_op jit(solution)/shard_map/encode_half/pallas_call | solution.py:61
  2.3 11.9 %all-to-all-start = ((bf16[32,32,256]{2,1,0:T(8,128)(2,1)}), bf16[32,32,256]{2,1,0:T(8,128)(2,1)S(1)}, u32[]{:S(2)}, u32[]{:S(2)}) async-start(bf16[32,32,256]{2,1,0:T(8,128)(2,1)} %encode_half.1), calls=%async_computation | async-start | bytes 1048576 | tf_op jit(solution)/shard_map/all_to_all | solution.py:31
  14.1 0.0 copy-done.1
  14.1 11.6 %all-gather.1 = s32[8,1,128]{2,1,0:T(1,128)S(1)} all-gather(s32[1,1,128]{2,1,0:T(1,128)S(1)} %bitcast.20), channel_id=2, replica_groups=mesh['z'=8,'x'=4,'y'=4,'core'=2] {'y','core'}, dimensions={0}, use_global_device_ids=true | all-gather | bytes 4608 | tf_op jit(solution)/shard_map/all_gather | solution.py:247
  25.7 4.7 %all-to-all-done = bf16[32,32,256]{2,1,0:T(8,128)(2,1)S(1)} async-done(((bf16[32,32,256]{2,1,0:T(8,128)(2,1)}), bf16[32,32,256]{2,1,0:T(8,128)(2,1)S(1)}, u32[]{:S(2)}, u32[]{:S(2)}) %all-to-all-start) | async-done | bytes 524320 | tf_op jit(solution)/shard_map/all_to_all | solution.py:31
  30.4 2.4 %collective-permute-start = (bf16[1024,256]{1,0:T(8,128)(2,1)S(1)}, bf16[1024,256]{1,0:T(8,128)(2,1)S(1)}, u32[]{:S(2)}, u32[]{:S(2)}) collective-permute-start(bf16[1024,256]{1,0:T(8,128)(2,1)S(1)} %bitcast.13), channel_id=1, source_target_pairs={{0,1},{1,0},{2,3},{3,2},{4,5},{5,4},{6,7},{7,6},{8,9},{9,8},{10,11... | collective-permute-start | bytes 1572872 | tf_op jit(solution)/shard_map/ppermute | solution.py:249
  32.8 1.5 %first_half.1 = (bf16[1024,256]{1,0:T(8,128)(2,1)S(1)}, bf16[3584,256]{1,0:T(8,128)(2,1)S(1)}) custom-call(s32[1]{0:T(128)} %bitcast.core_ref.side_ref, s32[8,128]{1,0:T(8,128)S(1)} %bitcast.15, bf16[1024,256]{1,0:T(8,128)(2,1)S(1)} %bitcast.14, bf16[3584,256]{1,0:T(8,128)(2,1)} %bitcast.17), custom_call_target="tpu_custom_call" | custom-call | tf_op jit(solution)/shard_map/first_half/pallas_call | solution.py:93
  34.4 0.0 collective-permute-done.other_ref
  34.4 0.8 %embed.1.embedded_ref = bf16[1024,256]{1,0:T(8,128)(2,1)S(1)} custom-call(s32[1]{0:T(128)} %bitcast.core_ref.side_ref, s32[8,128]{1,0:T(8,128)S(1)} %bitcast.16, bf16[1024,256]{1,0:T(8,128)(2,1)S(1)} %get-tuple-element.20.part_ref, bf16[1024,256]{1,0:T(8,128)(2,1)S(1)} %collective-permute-done.other_ref), custom_call_target="tpu_custom_call" | custom-call | tf_op jit(solution)/shard_map/embed/pallas_call | solution.py:112
  35.2 1.2 %squares.3 = f32[4,8,128]{2,1,0:T(8,128)S(1)} custom-call(s32[1]{0:T(128)S(6)} %sub.3.side_ref, bf16[1024,256]{1,0:T(8,128)(2,1)S(1)} %embed.1.embedded_ref, bf16[3584,256]{1,0:T(8,128)(2,1)S(1)} %get-tuple-element.19.weights_ref), custom_call_target="tpu_custom_call" | custom-call | tf_op jit(solution)/shard_map/squares/pallas_call | solution.py:140
  36.4 0.0 copy-start
  36.4 0.5 collective-permute-start.1
  36.9 1.2 %squares.2.keep_ref = f32[4,8,128]{2,1,0:T(8,128)S(1)} custom-call(s32[1]{0:T(128)} %bitcast.core_ref.side_ref, bf16[1024,256]{1,0:T(8,128)(2,1)S(1)} %embed.1.embedded_ref, bf16[3584,256]{1,0:T(8,128)(2,1)S(1)} %get-tuple-element.19.weights_ref), custom_call_target="tpu_custom_call" | custom-call | tf_op jit(solution)/shard_map/squares/pallas_call | solution.py:140
  38.0 0.0 collective-permute-done.1.received_ref
  38.1 1.4 %collective-permute-start.2 = (f32[8,128]{1,0:T(8,128)S(1)}, f32[8,128]{1,0:T(8,128)S(1)}, u32[]{:S(2)}, u32[]{:S(2)}) collective-permute-start(f32[8,128]{1,0:T(8,128)S(1)} %get-tuple-element.22), channel_id=1, source_target_pairs={{0,2},{2,4},{4,6},{6,0},{1,3},{3,5},{5,7},{7,1},{8,10},{10,12},{12... | collective-permute-start | bytes 12296 | tf_op jit(solution)/shard_map/ppermute | solution.py:188
  39.4 2.6 %collective-permute-start.3 = (f32[8,128]{1,0:T(8,128)S(1)}, f32[8,128]{1,0:T(8,128)S(1)}, u32[]{:S(2)}, u32[]{:S(2)}) collective-permute-start(f32[8,128]{1,0:T(8,128)S(1)} %get-tuple-element.23), channel_id=1, source_target_pairs={{0,4},{2,6},{4,0},{6,2},{1,5},{3,7},{5,1},{7,3},{8,12},{10,14},{12... | collective-permute-start | bytes 12296 | tf_op jit(solution)/shard_map/ppermute | solution.py:188
  42.1 1.1 %collective-permute-start.4 = (f32[8,128]{1,0:T(8,128)S(1)}, f32[8,128]{1,0:T(8,128)S(1)}, u32[]{:S(2)}, u32[]{:S(2)}) collective-permute-start(f32[8,128]{1,0:T(8,128)S(1)} %get-tuple-element.24), channel_id=1, source_target_pairs={{0,6},{2,0},{4,2},{6,4},{1,7},{3,1},{5,3},{7,5},{8,14},{10,8},{12,... | collective-permute-start | bytes 12296 | tf_op jit(solution)/shard_map/ppermute | solution.py:188
  43.1 0.0 collective-permute-done.2.refs_1_
  43.1 0.3 collective-permute-done.3.refs_2_
  43.4 1.2 %collective-permute-done.4.refs_3_ = f32[8,128]{1,0:T(8,128)S(1)} collective-permute-done((f32[8,128]{1,0:T(8,128)S(1)}, f32[8,128]{1,0:T(8,128)S(1)}, u32[]{:S(2)}, u32[]{:S(2)}) %collective-permute-start.4) | collective-permute-done | bytes 4128 | tf_op jit(solution)/shard_map/ppermute | solution.py:188
  44.6 13.5 %all_to_all.10 = f32[32,8,128]{2,1,0:T(8,128)S(1)} all-to-all(f32[32,8,128]{2,1,0:T(8,128)S(1)} %sum_for_each.1), channel_id=1, replica_groups=mesh['z'=8,'x'=4,'y'=4,'core'=2] {'z','x'}, dimensions={0} | all-to-all | bytes 262144 | tf_op jit(solution)/shard_map/all_to_all | solution.py:31
  58.1 3.4 %collective-permute-start.5 = (f32[8,128]{1,0:T(8,128)S(1)}, f32[8,128]{1,0:T(8,128)S(1)}, u32[]{:S(2)}, u32[]{:S(2)}) collective-permute-start(f32[8,128]{1,0:T(8,128)S(1)} %reduce_sum.9), channel_id=1, source_target_pairs={{0,1},{1,0},{2,3},{3,2},{4,5},{5,4},{6,7},{7,6},{8,9},{9,8},{10,11... | collective-permute-start | bytes 12296 | tf_op jit(solution)/shard_map/ppermute | solution.py:188
  61.5 0.8 %collective-permute-done.5 = f32[8,128]{1,0:T(8,128)S(1)} collective-permute-done((f32[8,128]{1,0:T(8,128)S(1)}, f32[8,128]{1,0:T(8,128)S(1)}, u32[]{:S(2)}, u32[]{:S(2)}) %collective-permute-start.5) | collective-permute-done | bytes 4128 | tf_op jit(solution)/shard_map/ppermute | solution.py:188
  62.3 2.2 %collective-permute-start.8 = (f32[2,8,128]{2,1,0:T(8,128)S(1)}, f32[2,8,128]{2,1,0:T(8,128)S(1)}, u32[]{:S(2)}, u32[]{:S(2)}) collective-permute-start(f32[2,8,128]{2,1,0:T(8,128)S(1)} %pad_maximum_fusion.refs_0_), channel_id=1, source_target_pairs={{0,6},{2,0},{4,2},{6,4},{1,7},{3,1},{5,3},{7,5},{8,14},{10,8},{12,... | collective-permute-start | bytes 24584 | tf_op jit(solution)/shard_map/ppermute | solution.py:188
  64.6 0.0 collective-permute-start.7
  64.6 0.6 collective-permute-start.6
  65.2 0.2 collective-permute-done.8.refs_3_
  65.4 3.2 %collective-permute-done.7.refs_2_ = f32[2,8,128]{2,1,0:T(8,128)S(1)} collective-permute-done((f32[2,8,128]{2,1,0:T(8,128)S(1)}, f32[2,8,128]{2,1,0:T(8,128)S(1)}, u32[]{:S(2)}, u32[]{:S(2)}) %collective-permute-start.7) | collective-permute-done | bytes 8224 | tf_op jit(solution)/shard_map/ppermute | solution.py:188
  68.6 0.0 collective-permute-done.6.refs_1_
  68.6 0.0 copy-done
  68.6 3.5 %scale.1 = bf16[3584,1024]{1,0:T(8,128)(2,1)} custom-call(s32[1]{0:T(128)} %bitcast.core_ref.side_ref, s32[1]{0:T(128)} %bitcast.1.row_ref, bf16[3584,256]{1,0:T(8,128)(2,1)S(1)} %get-tuple-element.19.weights_ref, bf16[1024,256]{1,0:T(8,128)(2,1)S(1)} %embed.1.embedded_ref, f32[2,8,128]{2,1,0:T(8,128)S(1)} %pad_maximum_fusion.refs_0_, ...), custom_call_target="tpu_custom_call" | custom-call | tf_op jit(solution)/shard_map/scale/pallas_call | solution.py:223
  (4 shorter events, 0.1 us)
Async XLA Ops:
  0.0 14.1 %copy-start.1 = (s32[128]{0:T(128)S(1)}, s32[128]{0:T(128)}, u32[]{:S(2)}) copy-start(s32[128]{0:T(128)} %param.6) | copy-start | bytes 1540
  2.3 28.2 %all-to-all-start = ((bf16[32,32,256]{2,1,0:T(8,128)(2,1)}), bf16[32,32,256]{2,1,0:T(8,128)(2,1)S(1)}, u32[]{:S(2)}, u32[]{:S(2)}) async-start(bf16[32,32,256]{2,1,0:T(8,128)(2,1)} %encode_half.1), calls=%async_computation | async-start | bytes 1048576 | tf_op jit(solution)/shard_map/all_to_all | solution.py:31
  30.4 4.0 %collective-permute-start = (bf16[1024,256]{1,0:T(8,128)(2,1)S(1)}, bf16[1024,256]{1,0:T(8,128)(2,1)S(1)}, u32[]{:S(2)}, u32[]{:S(2)}) collective-permute-start(bf16[1024,256]{1,0:T(8,128)(2,1)S(1)} %bitcast.13), channel_id=1, source_target_pairs={{0,1},{1,0},{2,3},{3,2},{4,5},{5,4},{6,7},{7,6},{8,9},{9,8},{10,11... | collective-permute-start | bytes 1572872 | tf_op jit(solution)/shard_map/ppermute | solution.py:249
  36.4 32.2 %copy-start = (bf16[8,448]{1,0:T(8,128)(2,1)S(1)}, bf16[8,448]{1,0:T(8,128)(2,1)}, u32[]{:S(2)}) copy-start(bf16[8,448]{1,0:T(8,128)(2,1)} %refs_4_.1) | copy-start | bytes 21508
  36.4 1.6 %collective-permute-start.1 = (f32[4,8,128]{2,1,0:T(8,128)S(1)}, f32[4,8,128]{2,1,0:T(8,128)S(1)}, u32[]{:S(2)}, u32[]{:S(2)}) collective-permute-start(f32[4,8,128]{2,1,0:T(8,128)S(1)} %squares.3), channel_id=1, source_target_pairs={{0,1},{1,0},{2,3},{3,2},{4,5},{5,4},{6,7},{7,6},{8,9},{9,8},{10,11... | collective-permute-start | bytes 49160 | tf_op jit(solution)/shard_map/ppermute | solution.py:188
  38.1 5.1 %collective-permute-start.2 = (f32[8,128]{1,0:T(8,128)S(1)}, f32[8,128]{1,0:T(8,128)S(1)}, u32[]{:S(2)}, u32[]{:S(2)}) collective-permute-start(f32[8,128]{1,0:T(8,128)S(1)} %get-tuple-element.22), channel_id=1, source_target_pairs={{0,2},{2,4},{4,6},{6,0},{1,3},{3,5},{5,7},{7,1},{8,10},{10,12},{12... | collective-permute-start | bytes 12296 | tf_op jit(solution)/shard_map/ppermute | solution.py:188
  39.4 4.0 %collective-permute-start.3 = (f32[8,128]{1,0:T(8,128)S(1)}, f32[8,128]{1,0:T(8,128)S(1)}, u32[]{:S(2)}, u32[]{:S(2)}) collective-permute-start(f32[8,128]{1,0:T(8,128)S(1)} %get-tuple-element.23), channel_id=1, source_target_pairs={{0,4},{2,6},{4,0},{6,2},{1,5},{3,7},{5,1},{7,3},{8,12},{10,14},{12... | collective-permute-start | bytes 12296 | tf_op jit(solution)/shard_map/ppermute | solution.py:188
  42.1 2.5 %collective-permute-start.4 = (f32[8,128]{1,0:T(8,128)S(1)}, f32[8,128]{1,0:T(8,128)S(1)}, u32[]{:S(2)}, u32[]{:S(2)}) collective-permute-start(f32[8,128]{1,0:T(8,128)S(1)} %get-tuple-element.24), channel_id=1, source_target_pairs={{0,6},{2,0},{4,2},{6,4},{1,7},{3,1},{5,3},{7,5},{8,14},{10,8},{12,... | collective-permute-start | bytes 12296 | tf_op jit(solution)/shard_map/ppermute | solution.py:188
  58.1 4.2 %collective-permute-start.5 = (f32[8,128]{1,0:T(8,128)S(1)}, f32[8,128]{1,0:T(8,128)S(1)}, u32[]{:S(2)}, u32[]{:S(2)}) collective-permute-start(f32[8,128]{1,0:T(8,128)S(1)} %reduce_sum.9), channel_id=1, source_target_pairs={{0,1},{1,0},{2,3},{3,2},{4,5},{5,4},{6,7},{7,6},{8,9},{9,8},{10,11... | collective-permute-start | bytes 12296 | tf_op jit(solution)/shard_map/ppermute | solution.py:188
  62.3 3.0 %collective-permute-start.8 = (f32[2,8,128]{2,1,0:T(8,128)S(1)}, f32[2,8,128]{2,1,0:T(8,128)S(1)}, u32[]{:S(2)}, u32[]{:S(2)}) collective-permute-start(f32[2,8,128]{2,1,0:T(8,128)S(1)} %pad_maximum_fusion.refs_0_), channel_id=1, source_target_pairs={{0,6},{2,0},{4,2},{6,4},{1,7},{3,1},{5,3},{7,5},{8,14},{10,8},{12,... | collective-permute-start | bytes 24584 | tf_op jit(solution)/shard_map/ppermute | solution.py:188
  64.6 4.0 %collective-permute-start.7 = (f32[2,8,128]{2,1,0:T(8,128)S(1)}, f32[2,8,128]{2,1,0:T(8,128)S(1)}, u32[]{:S(2)}, u32[]{:S(2)}) collective-permute-start(f32[2,8,128]{2,1,0:T(8,128)S(1)} %pad_maximum_fusion.refs_0_), channel_id=1, source_target_pairs={{0,4},{2,6},{4,0},{6,2},{1,5},{3,7},{5,1},{7,3},{8,12},{10,14},{12... | collective-permute-start | bytes 24584 | tf_op jit(solution)/shard_map/ppermute | solution.py:188
  64.6 4.0 %collective-permute-start.6 = (f32[2,8,128]{2,1,0:T(8,128)S(1)}, f32[2,8,128]{2,1,0:T(8,128)S(1)}, u32[]{:S(2)}, u32[]{:S(2)}) collective-permute-start(f32[2,8,128]{2,1,0:T(8,128)S(1)} %pad_maximum_fusion.refs_0_), channel_id=1, source_target_pairs={{0,2},{2,4},{4,6},{6,0},{1,3},{3,5},{5,7},{7,1},{8,10},{10,12},{12... | collective-permute-start | bytes 24584 | tf_op jit(solution)/shard_map/ppermute | solution.py:188

commit v4 on v3

--- a/solution.py
+++ b/solution.py
@@ -10,6 +10,8 @@
 PARAM = ("z", "x")
 TASK = ("y", "core")
 PARAM_TASK = ("z", "x", "y", "core")
+PLANE = ("x", "y")
+COLUMN = "z"
 LANES = 128
 EPSILON = 1e-06
 
@@ -147,40 +149,38 @@
     )(side, embedded, weights)
 
 
-def split_by_row(row, keep, received):
-    count = keep.shape[0]
-
-    def kernel(row_ref, keep_ref, received_ref, *out_refs):
-        for ahead, out_ref in enumerate(out_refs):
-            chunk = lax.rem(row_ref[0] + ahead, count)
-            out_ref[...] = keep_ref[chunk] + received_ref[chunk]
-
-    return pl.pallas_call(
-        kernel,
-        out_shape=[jax.ShapeDtypeStruct(keep.shape[1:], jnp.float32)] * count,
-        in_specs=[SMEM, VMEM, VMEM],
-        out_specs=[VMEM] * count,
-        compiler_params=limit(4),
-        name="split_by_row",
-    )(row, keep, received)
-
-
 def sum_for_each(pieces, copies):
-    def kernel(*refs):
-        total = refs[0][...]
-        for piece_ref in refs[1:-1]:
-            total = total + piece_ref[...]
+    def kernel(pieces_ref, out_ref):
+        total = pieces_ref[0]
+        for i in range(1, pieces_ref.shape[0]):
+            total = total + pieces_ref[i]
         for copy in range(copies):
-            refs[-1][copy] = total
-
-    return pl.pallas_call(
-        kernel,
-        out_shape=jax.ShapeDtypeStruct((copies, *pieces[0].shape), jnp.float32),
-        in_specs=[VMEM] * len(pieces),
-        out_specs=VMEM,
-        compiler_params=limit(4),
+            out_ref[copy] = total
+
+    return pl.pallas_call(
+        kernel,
+        out_shape=jax.ShapeDtypeStruct((copies, *pieces.shape[1:]), jnp.float32),
+        in_specs=[VMEM],
+        out_specs=VMEM,
+        compiler_params=limit(8),
         name="sum_for_each",
-    )(*pieces)
+    )(pieces)
+
+
+def pair_for_each(kept, received, copies):
+    def kernel(kept_ref, received_ref, out_ref):
+        total = kept_ref[...] + received_ref[...]
+        for copy in range(copies):
+            out_ref[copy] = total
+
+    return pl.pallas_call(
+        kernel,
+        out_shape=jax.ShapeDtypeStruct((copies, *kept.shape), jnp.float32),
+        in_specs=[VMEM, VMEM],
+        out_specs=VMEM,
+        compiler_params=limit(8),
+        name="pair_for_each",
+    )(kept, received)
 
 
 def around(x, axis, ahead):
@@ -188,58 +188,59 @@
     return lax.ppermute(x, axis, [(i, (i + ahead) % size) for i in range(size)])
 
 
-def scaled_adapters(core, row, weights, embedded, pairs, gain):
-    rows_of_chips = len(pairs)
+def scaled_adapters(side, weights, embedded, totals, gain, before=None):
     groups, columns = gain.shape
-    tasks, width = embedded.shape
+    chunks = totals.shape[0]
+    tasks = chunks * LANES
     padding = -columns % LANES
 
-    def kernel(core_ref, row_ref, weights_ref, embedded_ref, *refs):
-        pair_refs, (gain_ref, out_hbm, out_ref, totals_ref, sems) = refs[:rows_of_chips], refs[rows_of_chips:]
-        for behind in range(rows_of_chips):
-            chunk = lax.rem(row_ref[0] + rows_of_chips - behind, rows_of_chips)
-            totals_ref[core_ref[0] * rows_of_chips + chunk] = pair_refs[behind][0]
-            totals_ref[(1 - core_ref[0]) * rows_of_chips + chunk] = pair_refs[behind][1]
+    def kernel(side_ref, weights_ref, embedded_ref, totals_ref, gain_ref, *refs):
+        out_hbm, out_ref, sems = refs[-3:]
+        start = pl.multiple_of(side_ref[0] * tasks, tasks)
+        wanted = embedded_ref[pl.ds(start, tasks), :]
         gains = gain_ref[...].astype(jnp.float32)
         gains = jnp.transpose(jnp.concatenate([gains, jnp.zeros((groups, padding), jnp.float32)], axis=1))
         stores = []
         for g in range(groups):
-            rows = pl.ds(g * columns, columns)
-            power = jnp.concatenate([totals_ref[k, g : g + 1, :] for k in range(2 * rows_of_chips)], axis=1)
+            power = jnp.concatenate([totals_ref[k, g : g + 1, :] for k in range(chunks)], axis=1)
             inverse = lax.rsqrt(power / BLOCK + EPSILON)
             made = lax.dot_general(
                 weights_ref[g * columns : (g + 1) * columns, :],
-                embedded_ref[...],
+                wanted,
                 ROWS_BY_ROWS,
                 preferred_element_type=jnp.float32,
             )
             out_ref[g] = (made * inverse * gains[:columns, g : g + 1]).astype(jnp.bfloat16)
-            store = pltpu.make_async_copy(out_ref.at[g], out_hbm.at[rows, :], sems.at[g])
+            place = out_hbm.at[pl.ds(g * columns, columns), pl.ds(start, tasks)]
+            store = pltpu.make_async_copy(out_ref.at[g], place, sems.at[g])
             store.start()
             stores.append(store)
         for store in stores:
             store.wait()
 
-    return pl.pallas_call(
-        kernel,
-        out_shape=jax.ShapeDtypeStruct((groups * columns, tasks), jnp.bfloat16),
-        in_specs=[SMEM, SMEM] + [VMEM] * (3 + len(pairs)),
+    operands = [side, weights, embedded, totals, gain]
+    specs = [SMEM, VMEM, VMEM, VMEM, VMEM]
+    aliases = {}
+    if before is not None:
+        aliases = {len(operands): 0}
+        operands.append(before)
+        specs.append(HBM)
+    return pl.pallas_call(
+        kernel,
+        out_shape=jax.ShapeDtypeStruct((groups * columns, embedded.shape[0]), jnp.bfloat16),
+        in_specs=specs,
         out_specs=HBM,
-        scratch_shapes=[
-            pltpu.VMEM((groups, columns, tasks), jnp.bfloat16),
-            pltpu.VMEM((2 * rows_of_chips, groups, LANES), jnp.float32),
-            pltpu.SemaphoreType.DMA((groups,)),
-        ],
-        compiler_params=limit(24),
+        scratch_shapes=[pltpu.VMEM((groups, columns, tasks), jnp.bfloat16), pltpu.SemaphoreType.DMA((groups,))],
+        input_output_aliases=aliases,
+        compiler_params=limit(16),
         name="scale",
-    )(core, row, weights, embedded, *pairs, gain)
+    )(*operands)
 
 
 def on_device(task_ids, task_table, enc_in, enc_out, generator, gain):
     width, groups, columns = generator.shape
     half = task_table.shape[0] // 2
     core = lax.axis_index("core").reshape(1).astype(jnp.int32)
-    row = lax.axis_index("y").reshape(1).astype(jnp.int32)
     weights = generator.transpose(1, 2, 0).reshape(groups * columns, width)
     copies = encode_half(core, task_table, enc_in, enc_out, lax.axis_size(PARAM))
     task_ids, copies = lax.optimization_barrier((task_ids, copies))
@@ -252,13 +253,12 @@
     given = squares_of(1 - core, embedded, weights, groups)
     received = around(given, "core", 1)
     kept = squares_of(core, embedded, weights, groups)
-    own, *others = split_by_row(row, kept, received)
-    steps = range(1, len(others) + 1)
-    arrived = [around(piece, "y", ahead) for ahead, piece in zip(steps, others)]
-    totals = exchange(sum_for_each([own, *arrived], lax.axis_size(PARAM)), PARAM).sum(axis=0)
-    pair = jnp.stack([totals, around(totals, "core", 1)])
-    pairs = [pair] + [around(pair, "y", ahead) for ahead in steps]
-    made = scaled_adapters(core, row, weights, embedded, pairs, gain)
+    plane = exchange(pair_for_each(kept, received, lax.axis_size(PLANE)), PLANE)
+    column = exchange(sum_for_each(plane, lax.axis_size(COLUMN)), COLUMN)
+    totals = sum_for_each(column, 1)[0]
+    others = around(totals, "core", 1)
+    made = scaled_adapters(core, weights, embedded, totals, gain)
+    made = scaled_adapters(1 - core, weights, embedded, others, gain, made)
     return made.reshape(groups, columns, -1).transpose(2, 0, 1)
 
 

time: 72.4 us -> 69.9 us (0.965)
  blocking collectives: 25.1 us -> 35.8 us
  starting transfers between devices: 26 us -> 17.7 us
  waiting for transfers between devices: 10.4 us -> 4.53 us
  Pallas kernels: 10.5 us -> 11.6 us
    all_to_all x1 -> x2, blocking collectives: 13.5 us -> 24 us  [exchange(): return lax.all_to_all(x, axis, split_axis=0, concat_axis=0, tiled=True)]
    ppermute x8 -> x2, starting transfers between devices: 11.7 us -> 3.38 us  [around(): return lax.ppermute(x, axis, [(i, (i + ahead) % size) for i in range(size)])]
    ppermute x8 -> x2, waiting for transfers between devices: 5.7 us -> 0.01 us  [around(): return lax.ppermute(x, axis, [(i, (i + ahead) % size) for i in range(size)])]
    pallas_call x1 -> x2, Pallas kernels: 3.55 us -> 4.52 us  [scaled_adapters(): pl.pallas_call(kernel, out_shape=jax.ShapeDtypeStruct((groups * columns,...]
  transfers between devices with their start and end apart: 10 -> 4, of which waited for: 6 -> 1; matrix products, arithmetic and copies ran while one was open for 0% -> 0% of each run, Pallas kernels for 4% -> 7%
where the time goes in v4:
time: 69.9 us; the launch traced here: 69.6 us
  blocking collectives  35.8 us (51%)
  starting transfers between devices  17.7 us (25%)
  Pallas kernels  11.6 us (17%)
  waiting for transfers between devices  4.53 us (6%)
    all_to_all x2, blocking collectives, exchange(): return lax.all_to_all(x, axis, split_axis=0, concat_axis=0, tiled=True)  24 us
    all_to_all x1, starting transfers between devices, exchange(): return lax.all_to_all(x, axis, split_axis=0, concat_axis=0, tiled=True)  11.9 us
    all_gather x1, blocking collectives, on_device(): ids = lax.all_gather(task_ids.reshape(1, -1), TASK, axis=0, tiled=True)  11.8 us
    pallas_call x2, Pallas kernels, scaled_adapters(): pl.pallas_call(kernel, out_shape=jax.ShapeDtypeStruct((groups * columns,...  4.52 us
    all_to_all x1, waiting for transfers between devices, exchange(): return lax.all_to_all(x, axis, split_axis=0, concat_axis=0, tiled=True)  4.52 us
    ppermute x2, starting transfers between devices, around(): return lax.ppermute(x, axis, [(i, (i + ahead) % size) for i in range(size)])  3.38 us
    ppermute x1, starting transfers between devices, on_device(): other = lax.ppermute(mine, 'core', [(0, 1), (1, 0)])  2.43 us
    pallas_call x2, Pallas kernels, squares_of(): pl.pallas_call(kernel, out_shape=jax.ShapeDtypeStruct((chunks, groups, LA...  2.4 us
  transfers between devices with their start and end apart: 4, of which 1 were waited for; matrix products, arithmetic and copies ran while one was open for 0% of the time, Pallas kernels for 7%

profile of v4, /device:TPU:1, one launch (start us, length us, event | category | flops | bytes accessed | tf_op | source)
XLA Modules:
  0.0 69.6 jit_solution(18058535159222726370)
XLA Ops:
  0.0 0.0 copy-start
  0.0 2.2 %encode_half.1 = bf16[32,32,256]{2,1,0:T(8,128)(2,1)} custom-call(s32[1]{0:T(128)} %bitcast.core_ref.side_ref, bf16[64,256]{1,0:T(8,128)(2,1)} %table_hbm.1, bf16[256,512]{1,0:T(8,128)(2,1)} %enc_in_hbm.1, bf16[512,256]{1,0:T(8,128)(2,1)} %enc_out_hbm.1), custom_call_target="tpu_custom_call" | custom-call | tf_op jit(solution)/shard_map/encode_half/pallas_call | solution.py:63
  2.3 11.9 %all-to-all-start = ((bf16[32,32,256]{2,1,0:T(8,128)(2,1)}), bf16[32,32,256]{2,1,0:T(8,128)(2,1)S(1)}, u32[]{:S(2)}, u32[]{:S(2)}) async-start(bf16[32,32,256]{2,1,0:T(8,128)(2,1)} %encode_half.1), calls=%async_computation | async-start | bytes 1048576 | tf_op jit(solution)/shard_map/all_to_all | solution.py:33
  14.1 11.8 %all-gather.1 = s32[8,1,128]{2,1,0:T(1,128)S(1)} all-gather(s32[1,1,128]{2,1,0:T(1,128)} %bitcast.18), channel_id=2, replica_groups=mesh['z'=8,'x'=4,'y'=4,'core'=2] {'y','core'}, dimensions={0}, use_global_device_ids=true | all-gather | bytes 4608 | tf_op jit(solution)/shard_map/all_gather | solution.py:248
  25.9 4.5 %all-to-all-done = bf16[32,32,256]{2,1,0:T(8,128)(2,1)S(1)} async-done(((bf16[32,32,256]{2,1,0:T(8,128)(2,1)}), bf16[32,32,256]{2,1,0:T(8,128)(2,1)S(1)}, u32[]{:S(2)}, u32[]{:S(2)}) %all-to-all-start) | async-done | bytes 524320 | tf_op jit(solution)/shard_map/all_to_all | solution.py:33
  30.4 2.4 %collective-permute-start = (bf16[1024,256]{1,0:T(8,128)(2,1)S(1)}, bf16[1024,256]{1,0:T(8,128)(2,1)S(1)}, u32[]{:S(2)}, u32[]{:S(2)}) collective-permute-start(bf16[1024,256]{1,0:T(8,128)(2,1)S(1)} %bitcast.11), channel_id=1, source_target_pairs={{0,1},{1,0},{2,3},{3,2},{4,5},{5,4},{6,7},{7,6},{8,9},{9,8},{10,11... | collective-permute-start | bytes 1572872 | tf_op jit(solution)/shard_map/ppermute | solution.py:250
  32.8 1.5 %first_half.1 = (bf16[1024,256]{1,0:T(8,128)(2,1)S(1)}, bf16[3584,256]{1,0:T(8,128)(2,1)S(1)}) custom-call(s32[1]{0:T(128)} %bitcast.core_ref.side_ref, s32[8,128]{1,0:T(8,128)S(1)} %bitcast.15, bf16[1024,256]{1,0:T(8,128)(2,1)S(1)} %bitcast.12, bf16[3584,256]{1,0:T(8,128)(2,1)} %bitcast.17), custom_call_target="tpu_custom_call" | custom-call | tf_op jit(solution)/shard_map/first_half/pallas_call | solution.py:95
  34.4 0.0 collective-permute-done.other_ref
  34.4 0.8 %embed.1.embedded_ref = bf16[1024,256]{1,0:T(8,128)(2,1)S(1)} custom-call(s32[1]{0:T(128)} %bitcast.core_ref.side_ref, s32[8,128]{1,0:T(8,128)S(1)} %bitcast.16, bf16[1024,256]{1,0:T(8,128)(2,1)S(1)} %get-tuple-element.16.part_ref, bf16[1024,256]{1,0:T(8,128)(2,1)S(1)} %collective-permute-done.other_ref), custom_call_target="tpu_custom_call" | custom-call | tf_op jit(solution)/shard_map/embed/pallas_call | solution.py:114
  35.2 1.2 %squares.3 = f32[4,8,128]{2,1,0:T(8,128)S(1)} custom-call(s32[1]{0:T(128)S(6)} %sub.4.side_ref, bf16[1024,256]{1,0:T(8,128)(2,1)S(1)} %embed.1.embedded_ref, bf16[3584,256]{1,0:T(8,128)(2,1)S(1)} %get-tuple-element.15.weights_ref), custom_call_target="tpu_custom_call" | custom-call | tf_op jit(solution)/shard_map/squares/pallas_call | solution.py:142
  36.4 0.5 collective-permute-start.1
  36.9 1.2 %squares.2.kept_ref = f32[4,8,128]{2,1,0:T(8,128)S(1)} custom-call(s32[1]{0:T(128)} %bitcast.core_ref.side_ref, bf16[1024,256]{1,0:T(8,128)(2,1)S(1)} %embed.1.embedded_ref, bf16[3584,256]{1,0:T(8,128)(2,1)S(1)} %get-tuple-element.15.weights_ref), custom_call_target="tpu_custom_call" | custom-call | tf_op jit(solution)/shard_map/squares/pallas_call | solution.py:142
  38.1 0.0 collective-permute-done.1.received_ref
  38.1 13.7 %all_to_all.15.pieces_ref = f32[16,4,8,128]{3,2,1,0:T(8,128)S(1)} all-to-all(f32[16,4,8,128]{3,2,1,0:T(8,128)S(1)} %pair_for_each.1), channel_id=1, replica_groups=mesh['z'=8,'x'=4,'y'=4,'core'=2] {'x','y'}, dimensions={0} | all-to-all | bytes 524288 | tf_op jit(solution)/shard_map/all_to_all | solution.py:33
  51.8 10.3 %all_to_all.16.pieces_ref = f32[8,4,8,128]{3,2,1,0:T(8,128)S(1)} all-to-all(f32[8,4,8,128]{3,2,1,0:T(8,128)S(1)} %sum_for_each.2), channel_id=1, replica_groups=mesh['z'=8,'x'=4,'y'=4,'core'=2] {'z'}, dimensions={0} | all-to-all | bytes 262144 | tf_op jit(solution)/shard_map/all_to_all | solution.py:33
  62.2 2.9 %collective-permute-start.2 = (f32[4,8,128]{2,1,0:T(8,128)S(1)}, f32[4,8,128]{2,1,0:T(8,128)S(1)}, u32[]{:S(2)}, u32[]{:S(2)}) collective-permute-start(f32[4,8,128]{2,1,0:T(8,128)S(1)} %bitcast.13), channel_id=1, source_target_pairs={{0,1},{1,0},{2,3},{3,2},{4,5},{5,4},{6,7},{7,6},{8,9},{9,8},{10,11... | collective-permute-start | bytes 49160 | tf_op jit(solution)/shard_map/ppermute | solution.py:188
  65.1 0.0 copy-done
  65.1 2.3 %scale.2.refs_0_ = bf16[3584,1024]{1,0:T(8,128)(2,1)} custom-call(s32[1]{0:T(128)} %bitcast.core_ref.side_ref, bf16[3584,256]{1,0:T(8,128)(2,1)S(1)} %get-tuple-element.15.weights_ref, bf16[1024,256]{1,0:T(8,128)(2,1)S(1)} %embed.1.embedded_ref, f32[4,8,128]{2,1,0:T(8,128)S(1)} %bitcast.14, bf16[8,448]{1,0:T(8,128)(2,1)S(1)} %copy-done), custom_call_target="tpu_custom_call" | custom-call | tf_op jit(solution)/shard_map/scale/pallas_call | solution.py:228
  67.3 0.0 collective-permute-done.2.totals_ref
  67.4 2.3 %scale.3 = bf16[3584,1024]{1,0:T(8,128)(2,1)} custom-call(s32[1]{0:T(128)S(6)} %sub.4.side_ref, bf16[3584,256]{1,0:T(8,128)(2,1)S(1)} %get-tuple-element.15.weights_ref, bf16[1024,256]{1,0:T(8,128)(2,1)S(1)} %embed.1.embedded_ref, f32[4,8,128]{2,1,0:T(8,128)S(1)} %collective-permute-done.2.totals_ref, ...), custom_call_target="tpu_custom_call", output_to_operand_aliasing={{}: (5, {})} | custom-call | tf_op jit(solution)/shard_map/scale/pallas_call | solution.py:228
  (3 shorter events, 0.1 us)
Async XLA Ops:
  0.0 65.1 %copy-start = (bf16[8,448]{1,0:T(8,128)(2,1)S(1)}, bf16[8,448]{1,0:T(8,128)(2,1)}, u32[]{:S(2)}) copy-start(bf16[8,448]{1,0:T(8,128)(2,1)} %gain_ref.3) | copy-start | bytes 21508
  2.3 28.2 %all-to-all-start = ((bf16[32,32,256]{2,1,0:T(8,128)(2,1)}), bf16[32,32,256]{2,1,0:T(8,128)(2,1)S(1)}, u32[]{:S(2)}, u32[]{:S(2)}) async-start(bf16[32,32,256]{2,1,0:T(8,128)(2,1)} %encode_half.1), calls=%async_computation | async-start | bytes 1048576 | tf_op jit(solution)/shard_map/all_to_all | solution.py:33
  30.4 4.0 %collective-permute-start = (bf16[1024,256]{1,0:T(8,128)(2,1)S(1)}, bf16[1024,256]{1,0:T(8,128)(2,1)S(1)}, u32[]{:S(2)}, u32[]{:S(2)}) collective-permute-start(bf16[1024,256]{1,0:T(8,128)(2,1)S(1)} %bitcast.11), channel_id=1, source_target_pairs={{0,1},{1,0},{2,3},{3,2},{4,5},{5,4},{6,7},{7,6},{8,9},{9,8},{10,11... | collective-permute-start | bytes 1572872 | tf_op jit(solution)/shard_map/ppermute | solution.py:250
  36.4 1.7 %collective-permute-start.1 = (f32[4,8,128]{2,1,0:T(8,128)S(1)}, f32[4,8,128]{2,1,0:T(8,128)S(1)}, u32[]{:S(2)}, u32[]{:S(2)}) collective-permute-start(f32[4,8,128]{2,1,0:T(8,128)S(1)} %squares.3), channel_id=1, source_target_pairs={{0,1},{1,0},{2,3},{3,2},{4,5},{5,4},{6,7},{7,6},{8,9},{9,8},{10,11... | collective-permute-start | bytes 49160 | tf_op jit(solution)/shard_map/ppermute | solution.py:188
  62.2 5.2 %collective-permute-start.2 = (f32[4,8,128]{2,1,0:T(8,128)S(1)}, f32[4,8,128]{2,1,0:T(8,128)S(1)}, u32[]{:S(2)}, u32[]{:S(2)}) collective-permute-start(f32[4,8,128]{2,1,0:T(8,128)S(1)} %bitcast.13), channel_id=1, source_target_pairs={{0,1},{1,0},{2,3},{3,2},{4,5},{5,4},{6,7},{7,6},{8,9},{9,8},{10,11... | collective-permute-start | bytes 49160 | tf_op jit(solution)/shard_map/ppermute | solution.py:188

commit v5 on v4

--- a/solution.py
+++ b/solution.py
@@ -13,6 +13,7 @@
 PLANE = ("x", "y")
 COLUMN = "z"
 LANES = 128
+QUARTERS = 4
 EPSILON = 1e-06
 
 VMEM = pl.BlockSpec(memory_space=pltpu.VMEM)
@@ -37,9 +38,9 @@
     return exchange(jnp.broadcast_to(x, (lax.axis_size(axis), *x.shape)), axis)
 
 
-def encode_kernel(core_ref, table_hbm, enc_in_hbm, enc_out_hbm, out_ref, table_ref, enc_in_ref, enc_out_ref, sems):
+def encode_kernel(slot_ref, table_hbm, enc_in_hbm, enc_out_hbm, out_ref, table_ref, enc_in_ref, enc_out_ref, sems):
     copies, rows, _ = out_ref.shape
-    start = pl.multiple_of(core_ref[0] * rows, rows)
+    start = pl.multiple_of(slot_ref[0] * rows, rows)
     loads = [
         pltpu.make_async_copy(table_hbm.at[pl.ds(start, rows), :], table_ref, sems.at[0]),
         pltpu.make_async_copy(enc_in_hbm, enc_in_ref, sems.at[1]),
@@ -58,8 +59,8 @@
         out_ref[copy] = encoded
 
 
-def encode_half(core, task_table, enc_in, enc_out, copies):
-    rows, width = task_table.shape[0] // 2, task_table.shape[1]
+def encode_quarter(slot, task_table, enc_in, enc_out, copies):
+    rows, width = task_table.shape[0] // QUARTERS, task_table.shape[1]
     return pl.pallas_call(
         encode_kernel,
         out_shape=jax.ShapeDtypeStruct((copies, rows, width), jnp.bfloat16),
@@ -72,44 +73,78 @@
             pltpu.SemaphoreType.DMA((3,)),
         ],
         compiler_params=limit(8),
-        name="encode_half",
-    )(core, in_hbm(task_table), in_hbm(enc_in), in_hbm(enc_out))
-
-
-def picked_rows(ids_ref, part_ref, which, half):
+        name="encode_quarter",
+    )(slot, in_hbm(task_table), in_hbm(enc_in), in_hbm(enc_out))
+
+
+def split_in_two(x):
+    size = x.shape[0] // 2
+
+    def kernel(x_ref, low_ref, high_ref):
+        low_ref[...] = x_ref[:size]
+        high_ref[...] = x_ref[size:]
+
+    return pl.pallas_call(
+        kernel,
+        out_shape=[jax.ShapeDtypeStruct((size, *x.shape[1:]), x.dtype)] * 2,
+        in_specs=[VMEM],
+        out_specs=[VMEM, VMEM],
+        compiler_params=limit(4),
+        name="split_in_two",
+    )(x)
+
+
+def joined(low, high):
+    size = low.shape[0]
+
+    def kernel(low_ref, high_ref, out_ref):
+        out_ref[:size] = low_ref[...]
+        out_ref[size:] = high_ref[...]
+
+    return pl.pallas_call(
+        kernel,
+        out_shape=jax.ShapeDtypeStruct((2 * size, *low.shape[1:]), low.dtype),
+        in_specs=[VMEM, VMEM],
+        out_specs=VMEM,
+        compiler_params=limit(4),
+        name="joined",
+    )(low, high)
+
+
+def picked_rows(slot_ref, ids_ref, rows_ref, size):
     chunks = ids_ref.shape[0]
     ids = jnp.transpose(ids_ref[...])
-    place = lax.broadcasted_iota(jnp.int32, (1, part_ref.shape[0]), 1)
-    labels = (place // half) * (2 * half) + place % half + which * half
+    place = lax.broadcasted_iota(jnp.int32, (1, rows_ref.shape[0]), 1)
+    labels = (place // size) * (QUARTERS * size) + place % size + slot_ref[0] * size
     hot = [(ids[:, k : k + 1] == labels).astype(jnp.bfloat16) for k in range(chunks)]
-    return jnp.dot(jnp.concatenate(hot, axis=0), part_ref[...], preferred_element_type=jnp.float32)
-
-
-def first_half(core, ids, mine, weights, half):
-    def kernel(core_ref, ids_ref, mine_ref, weights_hbm, part_ref, weights_ref, sem):
+    return jnp.dot(jnp.concatenate(hot, axis=0), rows_ref[...], preferred_element_type=jnp.float32)
+
+
+def pick_first(slot, ids, rows, weights, size):
+    def kernel(slot_ref, ids_ref, rows_ref, weights_hbm, part_ref, weights_ref, sem):
         load = pltpu.make_async_copy(weights_hbm, weights_ref, sem)
         load.start()
-        part_ref[...] = picked_rows(ids_ref, mine_ref, core_ref[0], half).astype(jnp.bfloat16)
+        part_ref[...] = picked_rows(slot_ref, ids_ref, rows_ref, size).astype(jnp.bfloat16)
         load.wait()
 
     return pl.pallas_call(
         kernel,
         out_shape=(
-            jax.ShapeDtypeStruct((ids.size, mine.shape[1]), jnp.bfloat16),
+            jax.ShapeDtypeStruct((ids.size, rows.shape[1]), jnp.bfloat16),
             jax.ShapeDtypeStruct(weights.shape, weights.dtype),
         ),
         in_specs=[SMEM, VMEM, VMEM, HBM],
         out_specs=(VMEM, VMEM),
         scratch_shapes=[pltpu.SemaphoreType.DMA],
         compiler_params=limit(16),
-        name="first_half",
-    )(core, ids, mine, in_hbm(weights))
-
-
-def embed(core, ids, part, other, half):
-    def kernel(core_ref, ids_ref, part_ref, other_ref, embedded_ref):
-        rest = picked_rows(ids_ref, other_ref, 1 - core_ref[0], half)
-        embedded_ref[...] = (part_ref[...].astype(jnp.float32) + rest).astype(jnp.bfloat16)
+        name="pick_first",
+    )(slot, ids, rows, in_hbm(weights))
+
+
+def pick_more(slot, ids, rows, part, size):
+    def kernel(slot_ref, ids_ref, rows_ref, part_ref, out_ref):
+        more = picked_rows(slot_ref, ids_ref, rows_ref, size)
+        out_ref[...] = (part_ref[...].astype(jnp.float32) + more).astype(jnp.bfloat16)
 
     return pl.pallas_call(
         kernel,
@@ -117,8 +152,8 @@
         in_specs=[SMEM, VMEM, VMEM, VMEM],
         out_specs=VMEM,
         compiler_params=limit(16),
-        name="embed",
-    )(core, ids, part, other)
+        name="pick_more",
+    )(slot, ids, rows, part)
 
 
 def squares_of(side, embedded, weights, groups):
@@ -239,17 +274,25 @@
 
 def on_device(task_ids, task_table, enc_in, enc_out, generator, gain):
     width, groups, columns = generator.shape
-    half = task_table.shape[0] // 2
+    size = task_table.shape[0] // QUARTERS
     core = lax.axis_index("core").reshape(1).astype(jnp.int32)
+    parity = lax.axis_index("y").reshape(1).astype(jnp.int32) & 1
     weights = generator.transpose(1, 2, 0).reshape(groups * columns, width)
-    copies = encode_half(core, task_table, enc_in, enc_out, lax.axis_size(PARAM))
+    copies = encode_quarter(2 * core + parity, task_table, enc_in, enc_out, lax.axis_size(PARAM))
     task_ids, copies = lax.optimization_barrier((task_ids, copies))
     mine = exchange(copies, PARAM).reshape(-1, width)
     ids = lax.all_gather(task_ids.reshape(1, -1), TASK, axis=0, tiled=True)
     mine, ids = lax.optimization_barrier((mine, ids))
-    other = lax.ppermute(mine, "core", [(0, 1), (1, 0)])
-    part, weights = first_half(core, ids, mine, weights, half)
-    embedded = embed(core, ids, part, other, half)
+    low, high = split_in_two(mine)
+    low, high = around(low, "y", 1), around(high, "y", -1)
+    swapped = around(mine, "core", 1)
+    part, weights = pick_first(2 * core + parity, ids, mine, weights, size)
+    part = pick_more(2 * (1 - core) + parity, ids, swapped, part, size)
+    low, high, part = lax.optimization_barrier((low, high, part))
+    beside = joined(low, high)
+    far = around(beside, "core", 1)
+    part = pick_more(2 * core + 1 - parity, ids, beside, part, size)
+    embedded = pick_more(2 * (1 - core) + 1 - parity, ids, far, part, size)
     given = squares_of(1 - core, embedded, weights, groups)
     received = around(given, "core", 1)
     kept = squares_of(core, embedded, weights, groups)

time: 69.9 us -> 74.4 us (1.064)
  starting transfers between devices: 17.7 us -> 21.2 us
  blocking collectives: 35.8 us -> 38.4 us
  waiting for transfers between devices: 4.53 us -> 2.08 us
    ppermute x2 -> x6, starting transfers between devices: 3.38 us -> 9.36 us  [around(): return lax.ppermute(x, axis, [(i, (i + ahead) % size) for i in range(size)])]
    all_to_all x1, waiting for transfers between devices: 4.52 us -> 0.01 us  [exchange(): return lax.all_to_all(x, axis, split_axis=0, concat_axis=0, tiled=True)]
    all_to_all x2, blocking collectives: 24 us -> 26.7 us  [exchange(): return lax.all_to_all(x, axis, split_axis=0, concat_axis=0, tiled=True)]
    ppermute x1 -> x0, starting transfers between devices: 2.43 us -> none  [on_device(): other = lax.ppermute(mine, 'core', [(0, 1), (1, 0)])]
    ppermute x2 -> x6, waiting for transfers between devices: 0.01 us -> 2.08 us  [around(): return lax.ppermute(x, axis, [(i, (i + ahead) % size) for i in range(size)])]
    pallas_call x3 -> x7, Pallas kernels: 4.59 us -> 5.33 us  [the longest x1 2.11 us: encode_quarter(): pl.pallas_call(encode_kernel, out_shape=jax.ShapeDtypeStruct((copies, row...]
  transfers between devices with their start and end apart: 4 -> 7, of which waited for: 1 -> 2; matrix products, arithmetic and copies ran while one was open for 0% -> 0% of each run, Pallas kernels for 7% -> 8%
where the time goes in v5:
time: 74.4 us; the launch traced here: 74.2 us
  blocking collectives  38.4 us (52%)
  starting transfers between devices  21.2 us (28%)
  Pallas kernels  12.3 us (17%)
  waiting for transfers between devices  2.08 us (3%)
    all_to_all x2, blocking collectives, exchange(): return lax.all_to_all(x, axis, split_axis=0, concat_axis=0, tiled=True)  26.7 us
    all_to_all x1, starting transfers between devices, exchange(): return lax.all_to_all(x, axis, split_axis=0, concat_axis=0, tiled=True)  11.9 us
    all_gather x1, blocking collectives, on_device(): ids = lax.all_gather(task_ids.reshape(1, -1), TASK, axis=0, tiled=True)  11.8 us
    ppermute x6, starting transfers between devices, around(): return lax.ppermute(x, axis, [(i, (i + ahead) % size) for i in range(size)])  9.36 us
    pallas_call x2, Pallas kernels, scaled_adapters(): pl.pallas_call(kernel, out_shape=jax.ShapeDtypeStruct((groups * columns,...  4.53 us
    pallas_call x2, Pallas kernels, squares_of(): pl.pallas_call(kernel, out_shape=jax.ShapeDtypeStruct((chunks, groups, LA...  2.4 us
    pallas_call x1, Pallas kernels, encode_quarter(): pl.pallas_call(encode_kernel, out_shape=jax.ShapeDtypeStruct((copies, row...  2.11 us
    ppermute x6, waiting for transfers between devices, around(): return lax.ppermute(x, axis, [(i, (i + ahead) % size) for i in range(size)])  2.08 us
  transfers between devices with their start and end apart: 7, of which 2 were waited for; matrix products, arithmetic and copies ran while one was open for 0% of the time, Pallas kernels for 8%

profile of v5, /device:TPU:1, one launch (start us, length us, event | category | flops | bytes accessed | tf_op | source)
XLA Modules:
  0.0 74.2 jit_solution(2990199059760037627)
XLA Ops:
  0.0 0.0 copy-start
  0.0 2.1 %encode_quarter.1 = bf16[32,16,256]{2,1,0:T(8,128)(2,1)} custom-call(s32[1]{0:T(128)S(6)} %add.13.slot_ref, bf16[64,256]{1,0:T(8,128)(2,1)} %table_hbm.1, bf16[256,512]{1,0:T(8,128)(2,1)} %enc_in_hbm.1, bf16[512,256]{1,0:T(8,128)(2,1)} %enc_out_hbm.1), custom_call_target="tpu_custom_call" | custom-call | tf_op jit(solution)/shard_map/encode_quarter/pallas_call | solution.py:64
  2.1 11.9 %all-to-all-start = ((bf16[32,16,256]{2,1,0:T(8,128)(2,1)}), bf16[32,16,256]{2,1,0:T(8,128)(2,1)S(1)}, u32[]{:S(2)}, u32[]{:S(2)}) async-start(bf16[32,16,256]{2,1,0:T(8,128)(2,1)} %encode_quarter.1), calls=%async_computation | async-start | bytes 524288 | tf_op jit(solution)/shard_map/all_to_all | solution.py:34
  14.0 11.8 %all-gather.1 = s32[8,1,128]{2,1,0:T(1,128)S(1)} all-gather(s32[1,1,128]{2,1,0:T(1,128)} %bitcast.22), channel_id=2, replica_groups=mesh['z'=8,'x'=4,'y'=4,'core'=2] {'y','core'}, dimensions={0}, use_global_device_ids=true | all-gather | bytes 4608 | tf_op jit(solution)/shard_map/all_gather | solution.py:284
  25.8 0.0 all-to-all-done
  25.8 2.0 %collective-permute-start.2 = (bf16[512,256]{1,0:T(8,128)(2,1)S(1)}, bf16[512,256]{1,0:T(8,128)(2,1)S(1)}, u32[]{:S(2)}, u32[]{:S(2)}) collective-permute-start(bf16[512,256]{1,0:T(8,128)(2,1)S(1)} %bitcast.12), channel_id=1, source_target_pairs={{0,1},{1,0},{2,3},{3,2},{4,5},{5,4},{6,7},{7,6},{8,9},{9,8},{10,11... | collective-permute-start | bytes 786440 | tf_op jit(solution)/shard_map/ppermute | solution.py:223
  27.8 1.4 %collective-permute-start = (bf16[256,256]{1,0:T(8,128)(2,1)S(1)}, bf16[256,256]{1,0:T(8,128)(2,1)S(1)}, u32[]{:S(2)}, u32[]{:S(2)}) collective-permute-start(bf16[256,256]{1,0:T(8,128)(2,1)S(1)} %get-tuple-element.21), channel_id=1, source_target_pairs={{0,2},{2,4},{4,6},{6,0},{1,3},{3,5},{5,7},{7,1},{8,10},{10,12},{12... | collective-permute-start | bytes 393224 | tf_op jit(solution)/shard_map/ppermute | solution.py:223
  29.1 1.5 %collective-permute-start.1 = (bf16[256,256]{1,0:T(8,128)(2,1)S(1)}, bf16[256,256]{1,0:T(8,128)(2,1)S(1)}, u32[]{:S(2)}, u32[]{:S(2)}) collective-permute-start(bf16[256,256]{1,0:T(8,128)(2,1)S(1)} %get-tuple-element.22), channel_id=1, source_target_pairs={{0,6},{2,0},{4,2},{6,4},{1,7},{3,1},{5,3},{7,5},{8,14},{10,8},{12,... | collective-permute-start | bytes 393224 | tf_op jit(solution)/shard_map/ppermute | solution.py:223
  30.7 1.5 %pick_first.1 = (bf16[1024,256]{1,0:T(8,128)(2,1)S(1)}, bf16[3584,256]{1,0:T(8,128)(2,1)S(1)}) custom-call(s32[1]{0:T(128)S(6)} %add.13.slot_ref, s32[8,128]{1,0:T(8,128)S(1)} %bitcast.15, bf16[512,256]{1,0:T(8,128)(2,1)S(1)} %bitcast.14, bf16[3584,256]{1,0:T(8,128)(2,1)} %bitcast.21), custom_call_target="tpu_custom_call" | custom-call | tf_op jit(solution)/shard_map/pick_first/pallas_call | solution.py:130
  32.2 0.0 collective-permute-done.2.rows_ref
  32.2 0.6 pick_more.3.part_ref
  32.8 1.5 %collective-permute-done.low_ref = bf16[256,256]{1,0:T(8,128)(2,1)S(1)} collective-permute-done((bf16[256,256]{1,0:T(8,128)(2,1)S(1)}, bf16[256,256]{1,0:T(8,128)(2,1)S(1)}, u32[]{:S(2)}, u32[]{:S(2)}) %collective-permute-start) | collective-permute-done | bytes 131104 | tf_op jit(solution)/shard_map/ppermute | solution.py:223
  34.2 0.0 collective-permute-done.1.high_ref
  34.3 0.9 %collective-permute-start.3 = (bf16[512,256]{1,0:T(8,128)(2,1)S(1)}, bf16[512,256]{1,0:T(8,128)(2,1)S(1)}, u32[]{:S(2)}, u32[]{:S(2)}) collective-permute-start(bf16[512,256]{1,0:T(8,128)(2,1)S(1)} %joined.1.rows_ref), channel_id=1, source_target_pairs={{0,1},{1,0},{2,3},{3,2},{4,5},{5,4},{6,7},{7,6},{8,9},{9,8},{10,11... | collective-permute-start | bytes 786440 | tf_op jit(solution)/shard_map/ppermute | solution.py:223
  35.2 0.6 pick_more.4.part_ref
  35.7 0.6 collective-permute-done.3.rows_ref
  36.3 0.6 pick_more.5.embedded_ref
  36.9 1.2 %squares.3 = f32[4,8,128]{2,1,0:T(8,128)S(1)} custom-call(s32[1]{0:T(128)S(6)} %sub.12.side_ref, bf16[1024,256]{1,0:T(8,128)(2,1)S(1)} %pick_more.5.embedded_ref, bf16[3584,256]{1,0:T(8,128)(2,1)S(1)} %get-tuple-element.20.weights_ref), custom_call_target="tpu_custom_call" | custom-call | tf_op jit(solution)/shard_map/squares/pallas_call | solution.py:177
  38.1 0.5 collective-permute-start.4
  38.6 1.2 %squares.2.kept_ref = f32[4,8,128]{2,1,0:T(8,128)S(1)} custom-call(s32[1]{0:T(128)} %bitcast.side_ref, bf16[1024,256]{1,0:T(8,128)(2,1)S(1)} %pick_more.5.embedded_ref, bf16[3584,256]{1,0:T(8,128)(2,1)S(1)} %get-tuple-element.20.weights_ref), custom_call_target="tpu_custom_call" | custom-call | tf_op jit(solution)/shard_map/squares/pallas_call | solution.py:177
  39.8 0.0 collective-permute-done.4.received_ref
  39.8 12.8 %all_to_all.15.pieces_ref = f32[16,4,8,128]{3,2,1,0:T(8,128)S(1)} all-to-all(f32[16,4,8,128]{3,2,1,0:T(8,128)S(1)} %pair_for_each.1), channel_id=1, replica_groups=mesh['z'=8,'x'=4,'y'=4,'core'=2] {'x','y'}, dimensions={0} | all-to-all | bytes 524288 | tf_op jit(solution)/shard_map/all_to_all | solution.py:34
  52.7 13.8 %all_to_all.16.pieces_ref = f32[8,4,8,128]{3,2,1,0:T(8,128)S(1)} all-to-all(f32[8,4,8,128]{3,2,1,0:T(8,128)S(1)} %sum_for_each.2), channel_id=1, replica_groups=mesh['z'=8,'x'=4,'y'=4,'core'=2] {'z'}, dimensions={0} | all-to-all | bytes 262144 | tf_op jit(solution)/shard_map/all_to_all | solution.py:34
  66.5 3.1 %collective-permute-start.5 = (f32[4,8,128]{2,1,0:T(8,128)S(1)}, f32[4,8,128]{2,1,0:T(8,128)S(1)}, u32[]{:S(2)}, u32[]{:S(2)}) collective-permute-start(f32[4,8,128]{2,1,0:T(8,128)S(1)} %bitcast.19), channel_id=1, source_target_pairs={{0,1},{1,0},{2,3},{3,2},{4,5},{5,4},{6,7},{7,6},{8,9},{9,8},{10,11... | collective-permute-start | bytes 49160 | tf_op jit(solution)/shard_map/ppermute | solution.py:223
  69.6 0.0 copy-done
  69.6 2.3 %scale.2.refs_0_ = bf16[3584,1024]{1,0:T(8,128)(2,1)} custom-call(s32[1]{0:T(128)} %bitcast.side_ref, bf16[3584,256]{1,0:T(8,128)(2,1)S(1)} %get-tuple-element.20.weights_ref, bf16[1024,256]{1,0:T(8,128)(2,1)S(1)} %pick_more.5.embedded_ref, f32[4,8,128]{2,1,0:T(8,128)S(1)} %bitcast.20, bf16[8,448]{1,0:T(8,128)(2,1)S(1)} %copy-done), custom_call_target="tpu_custom_call" | custom-call | tf_op jit(solution)/shard_map/scale/pallas_call | solution.py:263
  71.9 0.0 collective-permute-done.5.totals_ref
  71.9 2.3 %scale.3 = bf16[3584,1024]{1,0:T(8,128)(2,1)} custom-call(s32[1]{0:T(128)S(6)} %sub.12.side_ref, bf16[3584,256]{1,0:T(8,128)(2,1)S(1)} %get-tuple-element.20.weights_ref, bf16[1024,256]{1,0:T(8,128)(2,1)S(1)} %pick_more.5.embedded_ref, f32[4,8,128]{2,1,0:T(8,128)S(1)} %collective-permute-done.5.totals_ref, ...), custom_call_target="tpu_custom_call", output_to_operand_aliasing={{}: (5, {})} | custom-call | tf_op jit(solution)/shard_map/scale/pallas_call | solution.py:263
  (5 shorter events, 0.1 us)
Async XLA Ops:
  0.0 69.6 %copy-start = (bf16[8,448]{1,0:T(8,128)(2,1)S(1)}, bf16[8,448]{1,0:T(8,128)(2,1)}, u32[]{:S(2)}) copy-start(bf16[8,448]{1,0:T(8,128)(2,1)} %gain_ref.3) | copy-start | bytes 21508
  2.1 23.6 %all-to-all-start = ((bf16[32,16,256]{2,1,0:T(8,128)(2,1)}), bf16[32,16,256]{2,1,0:T(8,128)(2,1)S(1)}, u32[]{:S(2)}, u32[]{:S(2)}) async-start(bf16[32,16,256]{2,1,0:T(8,128)(2,1)} %encode_quarter.1), calls=%async_computation | async-start | bytes 524288 | tf_op jit(solution)/shard_map/all_to_all | solution.py:34
  25.8 6.4 %collective-permute-start.2 = (bf16[512,256]{1,0:T(8,128)(2,1)S(1)}, bf16[512,256]{1,0:T(8,128)(2,1)S(1)}, u32[]{:S(2)}, u32[]{:S(2)}) collective-permute-start(bf16[512,256]{1,0:T(8,128)(2,1)S(1)} %bitcast.12), channel_id=1, source_target_pairs={{0,1},{1,0},{2,3},{3,2},{4,5},{5,4},{6,7},{7,6},{8,9},{9,8},{10,11... | collective-permute-start | bytes 786440 | tf_op jit(solution)/shard_map/ppermute | solution.py:223
  27.8 6.5 %collective-permute-start = (bf16[256,256]{1,0:T(8,128)(2,1)S(1)}, bf16[256,256]{1,0:T(8,128)(2,1)S(1)}, u32[]{:S(2)}, u32[]{:S(2)}) collective-permute-start(bf16[256,256]{1,0:T(8,128)(2,1)S(1)} %get-tuple-element.21), channel_id=1, source_target_pairs={{0,2},{2,4},{4,6},{6,0},{1,3},{3,5},{5,7},{7,1},{8,10},{10,12},{12... | collective-permute-start | bytes 393224 | tf_op jit(solution)/shard_map/ppermute | solution.py:223
  29.1 5.1 %collective-permute-start.1 = (bf16[256,256]{1,0:T(8,128)(2,1)S(1)}, bf16[256,256]{1,0:T(8,128)(2,1)S(1)}, u32[]{:S(2)}, u32[]{:S(2)}) collective-permute-start(bf16[256,256]{1,0:T(8,128)(2,1)S(1)} %get-tuple-element.22), channel_id=1, source_target_pairs={{0,6},{2,0},{4,2},{6,4},{1,7},{3,1},{5,3},{7,5},{8,14},{10,8},{12,... | collective-permute-start | bytes 393224 | tf_op jit(solution)/shard_map/ppermute | solution.py:223
  34.3 2.1 %collective-permute-start.3 = (bf16[512,256]{1,0:T(8,128)(2,1)S(1)}, bf16[512,256]{1,0:T(8,128)(2,1)S(1)}, u32[]{:S(2)}, u32[]{:S(2)}) collective-permute-start(bf16[512,256]{1,0:T(8,128)(2,1)S(1)} %joined.1.rows_ref), channel_id=1, source_target_pairs={{0,1},{1,0},{2,3},{3,2},{4,5},{5,4},{6,7},{7,6},{8,9},{9,8},{10,11... | collective-permute-start | bytes 786440 | tf_op jit(solution)/shard_map/ppermute | solution.py:223
  38.1 1.7 %collective-permute-start.4 = (f32[4,8,128]{2,1,0:T(8,128)S(1)}, f32[4,8,128]{2,1,0:T(8,128)S(1)}, u32[]{:S(2)}, u32[]{:S(2)}) collective-permute-start(f32[4,8,128]{2,1,0:T(8,128)S(1)} %squares.3), channel_id=1, source_target_pairs={{0,1},{1,0},{2,3},{3,2},{4,5},{5,4},{6,7},{7,6},{8,9},{9,8},{10,11... | collective-permute-start | bytes 49160 | tf_op jit(solution)/shard_map/ppermute | solution.py:223
  66.5 5.4 %collective-permute-start.5 = (f32[4,8,128]{2,1,0:T(8,128)S(1)}, f32[4,8,128]{2,1,0:T(8,128)S(1)}, u32[]{:S(2)}, u32[]{:S(2)}) collective-permute-start(f32[4,8,128]{2,1,0:T(8,128)S(1)} %bitcast.19), channel_id=1, source_target_pairs={{0,1},{1,0},{2,3},{3,2},{4,5},{5,4},{6,7},{7,6},{8,9},{9,8},{10,11... | collective-permute-start | bytes 49160 | tf_op jit(solution)/shard_map/ppermute | solution.py:223

commit v6 on v4

--- a/solution.py
+++ b/solution.py
@@ -76,49 +76,62 @@
     )(core, in_hbm(task_table), in_hbm(enc_in), in_hbm(enc_out))
 
 
-def picked_rows(ids_ref, part_ref, which, half):
-    chunks = ids_ref.shape[0]
-    ids = jnp.transpose(ids_ref[...])
-    place = lax.broadcasted_iota(jnp.int32, (1, part_ref.shape[0]), 1)
-    labels = (place // half) * (2 * half) + place % half + which * half
-    hot = [(ids[:, k : k + 1] == labels).astype(jnp.bfloat16) for k in range(chunks)]
-    return jnp.dot(jnp.concatenate(hot, axis=0), part_ref[...], preferred_element_type=jnp.float32)
-
-
-def first_half(core, ids, mine, weights, half):
-    def kernel(core_ref, ids_ref, mine_ref, weights_hbm, part_ref, weights_ref, sem):
-        load = pltpu.make_async_copy(weights_hbm, weights_ref, sem)
+def loaded(weights, after):
+    def kernel(weights_hbm, after_ref, out_ref, sem):
+        load = pltpu.make_async_copy(weights_hbm, out_ref, sem)
         load.start()
-        part_ref[...] = picked_rows(ids_ref, mine_ref, core_ref[0], half).astype(jnp.bfloat16)
         load.wait()
 
     return pl.pallas_call(
         kernel,
-        out_shape=(
-            jax.ShapeDtypeStruct((ids.size, mine.shape[1]), jnp.bfloat16),
-            jax.ShapeDtypeStruct(weights.shape, weights.dtype),
-        ),
-        in_specs=[SMEM, VMEM, VMEM, HBM],
-        out_specs=(VMEM, VMEM),
+        out_shape=jax.ShapeDtypeStruct(weights.shape, weights.dtype),
+        in_specs=[HBM, VMEM],
+        out_specs=VMEM,
         scratch_shapes=[pltpu.SemaphoreType.DMA],
+        compiler_params=limit(8),
+        name="loaded",
+    )(in_hbm(weights), after)
+
+
+def split_in_two(x):
+    size = x.shape[0] // 2
+
+    def kernel(x_ref, low_ref, high_ref):
+        low_ref[...] = x_ref[:size]
+        high_ref[...] = x_ref[size:]
+
+    return pl.pallas_call(
+        kernel,
+        out_shape=[jax.ShapeDtypeStruct((size, *x.shape[1:]), x.dtype)] * 2,
+        in_specs=[VMEM],
+        out_specs=[VMEM, VMEM],
+        compiler_params=limit(4),
+        name="split_in_two",
+    )(x)
+
+
+def picked(core, ids, rows, half, offset=0, part=None):
+    chunks = ids.shape[0]
+
+    def kernel(core_ref, ids_ref, rows_ref, *refs):
+        turned = jnp.transpose(ids_ref[...])
+        place = offset + lax.broadcasted_iota(jnp.int32, (1, rows_ref.shape[0]), 1)
+        labels = (place // half) * (2 * half) + place % half + core_ref[0] * half
+        hot = [(turned[:, k : k + 1] == labels).astype(jnp.bfloat16) for k in range(chunks)]
+        found = jnp.dot(jnp.concatenate(hot, axis=0), rows_ref[...], preferred_element_type=jnp.float32)
+        if part is not None:
+            found = found + refs[0][...].astype(jnp.float32)
+        refs[-1][...] = found.astype(jnp.bfloat16)
+
+    operands = [core, ids, rows] + ([] if part is None else [part])
+    return pl.pallas_call(
+        kernel,
+        out_shape=jax.ShapeDtypeStruct((ids.size, rows.shape[1]), jnp.bfloat16),
+        in_specs=[SMEM] + [VMEM] * (len(operands) - 1),
+        out_specs=VMEM,
         compiler_params=limit(16),
-        name="first_half",
-    )(core, ids, mine, in_hbm(weights))
-
-
-def embed(core, ids, part, other, half):
-    def kernel(core_ref, ids_ref, part_ref, other_ref, embedded_ref):
-        rest = picked_rows(ids_ref, other_ref, 1 - core_ref[0], half)
-        embedded_ref[...] = (part_ref[...].astype(jnp.float32) + rest).astype(jnp.bfloat16)
-
-    return pl.pallas_call(
-        kernel,
-        out_shape=jax.ShapeDtypeStruct(part.shape, jnp.bfloat16),
-        in_specs=[SMEM, VMEM, VMEM, VMEM],
-        out_specs=VMEM,
-        compiler_params=limit(16),
-        name="embed",
-    )(core, ids, part, other)
+        name="picked",
+    )(*operands)
 
 
 def squares_of(side, embedded, weights, groups):
@@ -246,10 +259,13 @@
     task_ids, copies = lax.optimization_barrier((task_ids, copies))
     mine = exchange(copies, PARAM).reshape(-1, width)
     ids = lax.all_gather(task_ids.reshape(1, -1), TASK, axis=0, tiled=True)
-    mine, ids = lax.optimization_barrier((mine, ids))
-    other = lax.ppermute(mine, "core", [(0, 1), (1, 0)])
-    part, weights = first_half(core, ids, mine, weights, half)
-    embedded = embed(core, ids, part, other, half)
+    weights = loaded(weights, ids)
+    mine, ids, weights = lax.optimization_barrier((mine, ids, weights))
+    low, high = [around(piece, "core", 1) for piece in split_in_two(mine)]
+    part = picked(core, ids, mine, half)
+    part = picked(1 - core, ids, low, half, 0, part)
+    high, part = lax.optimization_barrier((high, part))
+    embedded = picked(1 - core, ids, high, half, low.shape[0], part)
     given = squares_of(1 - core, embedded, weights, groups)
     received = around(given, "core", 1)
     kept = squares_of(core, embedded, weights, groups)

time: 69.9 us -> 70.1 us (level)
  waiting for transfers between devices: 4.53 us -> 3.23 us
  Pallas kernels: 11.6 us -> 12.7 us
    ppermute x2 -> x4, starting transfers between devices: 3.38 us -> 5.99 us  [around(): return lax.ppermute(x, axis, [(i, (i + ahead) % size) for i in range(size)])]
    ppermute x1 -> x0, starting transfers between devices: 2.43 us -> none  [on_device(): other = lax.ppermute(mine, 'core', [(0, 1), (1, 0)])]
    all_to_all x1, waiting for transfers between devices: 4.52 us -> 2.99 us  [exchange(): return lax.all_to_all(x, axis, split_axis=0, concat_axis=0, tiled=True)]
    pallas_call x2 -> x5, Pallas kernels: 2.35 us -> 3.48 us  [the longest x3 1.93 us: picked(): pl.pallas_call(kernel, out_shape=jax.ShapeDtypeStruct((ids.size, rows.sha...]
  transfers between devices with their start and end apart: 4 -> 5, of which waited for: 1 -> 2; matrix products, arithmetic and copies ran while one was open for 0% -> 0% of each run, Pallas kernels for 7% -> 9%
where the time goes in v6:
time: 70.1 us; the launch traced here: 69.7 us
  blocking collectives  35.8 us (51%)
  starting transfers between devices  17.9 us (26%)
  Pallas kernels  12.7 us (18%)
  waiting for transfers between devices  3.23 us (5%)
    all_to_all x2, blocking collectives, exchange(): return lax.all_to_all(x, axis, split_axis=0, concat_axis=0, tiled=True)  24 us
    all_to_all x1, starting transfers between devices, exchange(): return lax.all_to_all(x, axis, split_axis=0, concat_axis=0, tiled=True)  11.9 us
    all_gather x1, blocking collectives, on_device(): ids = lax.all_gather(task_ids.reshape(1, -1), TASK, axis=0, tiled=True)  11.8 us
    ppermute x4, starting transfers between devices, around(): return lax.ppermute(x, axis, [(i, (i + ahead) % size) for i in range(size)])  5.99 us
    pallas_call x2, Pallas kernels, scaled_adapters(): pl.pallas_call(kernel, out_shape=jax.ShapeDtypeStruct((groups * columns,...  4.53 us
    all_to_all x1, waiting for transfers between devices, exchange(): return lax.all_to_all(x, axis, split_axis=0, concat_axis=0, tiled=True)  2.99 us
    pallas_call x2, Pallas kernels, squares_of(): pl.pallas_call(kernel, out_shape=jax.ShapeDtypeStruct((chunks, groups, LA...  2.41 us
    pallas_call x1, Pallas kernels, encode_half(): pl.pallas_call(encode_kernel, out_shape=jax.ShapeDtypeStruct((copies, row...  2.23 us
  transfers between devices with their start and end apart: 5, of which 2 were waited for; matrix products, arithmetic and copies ran while one was open for 0% of the time, Pallas kernels for 9%

profile of v6, /device:TPU:1, one launch (start us, length us, event | category | flops | bytes accessed | tf_op | source)
XLA Modules:
  0.0 69.7 jit_solution(12450294007396324327)
XLA Ops:
  0.0 2.2 %encode_half.1 = bf16[32,32,256]{2,1,0:T(8,128)(2,1)} custom-call(s32[1]{0:T(128)} %bitcast.core_ref.side_ref, bf16[64,256]{1,0:T(8,128)(2,1)} %table_hbm.1, bf16[256,512]{1,0:T(8,128)(2,1)} %enc_in_hbm.1, bf16[512,256]{1,0:T(8,128)(2,1)} %enc_out_hbm.1), custom_call_target="tpu_custom_call" | custom-call | tf_op jit(solution)/shard_map/encode_half/pallas_call | solution.py:63
  2.2 11.9 %all-to-all-start = ((bf16[32,32,256]{2,1,0:T(8,128)(2,1)}), bf16[32,32,256]{2,1,0:T(8,128)(2,1)S(1)}, u32[]{:S(2)}, u32[]{:S(2)}) async-start(bf16[32,32,256]{2,1,0:T(8,128)(2,1)} %encode_half.1), calls=%async_computation | async-start | bytes 1048576 | tf_op jit(solution)/shard_map/all_to_all | solution.py:33
  14.1 0.0 copy-start
  14.1 11.8 %all-gather.1 = s32[8,1,128]{2,1,0:T(1,128)S(1)} all-gather(s32[1,1,128]{2,1,0:T(1,128)} %bitcast.20), channel_id=2, replica_groups=mesh['z'=8,'x'=4,'y'=4,'core'=2] {'y','core'}, dimensions={0}, use_global_device_ids=true | all-gather | bytes 4608 | tf_op jit(solution)/shard_map/all_gather | solution.py:261
  25.9 1.5 %loaded.1.weights_ref = bf16[3584,256]{1,0:T(8,128)(2,1)S(1)} custom-call(bf16[3584,256]{1,0:T(8,128)(2,1)} %bitcast.19, s32[8,128]{1,0:T(8,128)S(1)} %bitcast.13), custom_call_target="tpu_custom_call" | custom-call | tf_op jit(solution)/shard_map/loaded/pallas_call | solution.py:85
  27.4 3.0 %all-to-all-done = bf16[32,32,256]{2,1,0:T(8,128)(2,1)S(1)} async-done(((bf16[32,32,256]{2,1,0:T(8,128)(2,1)}), bf16[32,32,256]{2,1,0:T(8,128)(2,1)S(1)}, u32[]{:S(2)}, u32[]{:S(2)}) %all-to-all-start) | async-done | bytes 524320 | tf_op jit(solution)/shard_map/all_to_all | solution.py:33
  30.4 2.5 %collective-permute-start.1 = (bf16[512,256]{1,0:T(8,128)(2,1)S(1)}, bf16[512,256]{1,0:T(8,128)(2,1)S(1)}, u32[]{:S(2)}, u32[]{:S(2)}) collective-permute-start(bf16[512,256]{1,0:T(8,128)(2,1)S(1)} %get-tuple-element.20), channel_id=1, source_target_pairs={{0,1},{1,0},{2,3},{3,2},{4,5},{5,4},{6,7},{7,6},{8,9},{9,8},{10,11... | collective-permute-start | bytes 786440 | tf_op jit(solution)/shard_map/ppermute | solution.py:201
  32.9 0.1 collective-permute-start
  33.0 0.8 %picked.3.refs_0_ = bf16[1024,256]{1,0:T(8,128)(2,1)S(1)} custom-call(s32[1]{0:T(128)} %bitcast.core_ref.side_ref, s32[8,128]{1,0:T(8,128)S(1)} %bitcast.14, bf16[1024,256]{1,0:T(8,128)(2,1)S(1)} %bitcast.12), custom_call_target="tpu_custom_call" | custom-call | tf_op jit(solution)/shard_map/picked/pallas_call | solution.py:127
  33.9 0.2 collective-permute-done.1.rows_ref
  34.1 0.6 picked.4.refs_0_
  34.7 0.0 collective-permute-done.rows_ref
  34.7 0.6 picked.5.embedded_ref
  35.2 1.2 %squares.3 = f32[4,8,128]{2,1,0:T(8,128)S(1)} custom-call(s32[1]{0:T(128)S(6)} %sub.2.core_ref.side_ref, bf16[1024,256]{1,0:T(8,128)(2,1)S(1)} %picked.5.embedded_ref, bf16[3584,256]{1,0:T(8,128)(2,1)S(1)} %loaded.1.weights_ref), custom_call_target="tpu_custom_call" | custom-call | tf_op jit(solution)/shard_map/squares/pallas_call | solution.py:155
  36.5 0.5 collective-permute-start.2
  36.9 1.2 %squares.2.kept_ref = f32[4,8,128]{2,1,0:T(8,128)S(1)} custom-call(s32[1]{0:T(128)} %bitcast.core_ref.side_ref, bf16[1024,256]{1,0:T(8,128)(2,1)S(1)} %picked.5.embedded_ref, bf16[3584,256]{1,0:T(8,128)(2,1)S(1)} %loaded.1.weights_ref), custom_call_target="tpu_custom_call" | custom-call | tf_op jit(solution)/shard_map/squares/pallas_call | solution.py:155
  38.1 0.0 collective-permute-done.2.received_ref
  38.2 13.7 %all_to_all.15.pieces_ref = f32[16,4,8,128]{3,2,1,0:T(8,128)S(1)} all-to-all(f32[16,4,8,128]{3,2,1,0:T(8,128)S(1)} %pair_for_each.1), channel_id=1, replica_groups=mesh['z'=8,'x'=4,'y'=4,'core'=2] {'x','y'}, dimensions={0} | all-to-all | bytes 524288 | tf_op jit(solution)/shard_map/all_to_all | solution.py:33
  51.9 10.3 %all_to_all.16.pieces_ref = f32[8,4,8,128]{3,2,1,0:T(8,128)S(1)} all-to-all(f32[8,4,8,128]{3,2,1,0:T(8,128)S(1)} %sum_for_each.2), channel_id=1, replica_groups=mesh['z'=8,'x'=4,'y'=4,'core'=2] {'z'}, dimensions={0} | all-to-all | bytes 262144 | tf_op jit(solution)/shard_map/all_to_all | solution.py:33
  62.2 2.9 %collective-permute-start.3 = (f32[4,8,128]{2,1,0:T(8,128)S(1)}, f32[4,8,128]{2,1,0:T(8,128)S(1)}, u32[]{:S(2)}, u32[]{:S(2)}) collective-permute-start(f32[4,8,128]{2,1,0:T(8,128)S(1)} %bitcast.17), channel_id=1, source_target_pairs={{0,1},{1,0},{2,3},{3,2},{4,5},{5,4},{6,7},{7,6},{8,9},{9,8},{10,11... | collective-permute-start | bytes 49160 | tf_op jit(solution)/shard_map/ppermute | solution.py:201
  65.1 0.0 copy-done
  65.1 2.3 %scale.2.refs_0_ = bf16[3584,1024]{1,0:T(8,128)(2,1)} custom-call(s32[1]{0:T(128)} %bitcast.core_ref.side_ref, bf16[3584,256]{1,0:T(8,128)(2,1)S(1)} %loaded.1.weights_ref, bf16[1024,256]{1,0:T(8,128)(2,1)S(1)} %picked.5.embedded_ref, f32[4,8,128]{2,1,0:T(8,128)S(1)} %bitcast.18, bf16[8,448]{1,0:T(8,128)(2,1)S(1)} %copy-done), custom_call_target="tpu_custom_call" | custom-call | tf_op jit(solution)/shard_map/scale/pallas_call | solution.py:241
  67.4 0.0 collective-permute-done.3.totals_ref
  67.4 2.3 %scale.3 = bf16[3584,1024]{1,0:T(8,128)(2,1)} custom-call(s32[1]{0:T(128)S(6)} %sub.2.core_ref.side_ref, bf16[3584,256]{1,0:T(8,128)(2,1)S(1)} %loaded.1.weights_ref, bf16[1024,256]{1,0:T(8,128)(2,1)S(1)} %picked.5.embedded_ref, f32[4,8,128]{2,1,0:T(8,128)S(1)} %collective-permute-done.3.totals_ref, ...), custom_call_target="tpu_custom_call", output_to_operand_aliasing={{}: (5, {})} | custom-call | tf_op jit(solution)/shard_map/scale/pallas_call | solution.py:241
  (4 shorter events, 0.1 us)
Async XLA Ops:
  2.2 28.2 %all-to-all-start = ((bf16[32,32,256]{2,1,0:T(8,128)(2,1)}), bf16[32,32,256]{2,1,0:T(8,128)(2,1)S(1)}, u32[]{:S(2)}, u32[]{:S(2)}) async-start(bf16[32,32,256]{2,1,0:T(8,128)(2,1)} %encode_half.1), calls=%async_computation | async-start | bytes 1048576 | tf_op jit(solution)/shard_map/all_to_all | solution.py:33
  14.1 51.0 %copy-start = (bf16[8,448]{1,0:T(8,128)(2,1)S(1)}, bf16[8,448]{1,0:T(8,128)(2,1)}, u32[]{:S(2)}) copy-start(bf16[8,448]{1,0:T(8,128)(2,1)} %gain_ref.3) | copy-start | bytes 21508
  30.4 3.7 %collective-permute-start.1 = (bf16[512,256]{1,0:T(8,128)(2,1)S(1)}, bf16[512,256]{1,0:T(8,128)(2,1)S(1)}, u32[]{:S(2)}, u32[]{:S(2)}) collective-permute-start(bf16[512,256]{1,0:T(8,128)(2,1)S(1)} %get-tuple-element.20), channel_id=1, source_target_pairs={{0,1},{1,0},{2,3},{3,2},{4,5},{5,4},{6,7},{7,6},{8,9},{9,8},{10,11... | collective-permute-start | bytes 786440 | tf_op jit(solution)/shard_map/ppermute | solution.py:201
  32.9 1.7 %collective-permute-start = (bf16[512,256]{1,0:T(8,128)(2,1)S(1)}, bf16[512,256]{1,0:T(8,128)(2,1)S(1)}, u32[]{:S(2)}, u32[]{:S(2)}) collective-permute-start(bf16[512,256]{1,0:T(8,128)(2,1)S(1)} %get-tuple-element.19), channel_id=1, source_target_pairs={{0,1},{1,0},{2,3},{3,2},{4,5},{5,4},{6,7},{7,6},{8,9},{9,8},{10,11... | collective-permute-start | bytes 786440 | tf_op jit(solution)/shard_map/ppermute | solution.py:201
  36.5 1.7 %collective-permute-start.2 = (f32[4,8,128]{2,1,0:T(8,128)S(1)}, f32[4,8,128]{2,1,0:T(8,128)S(1)}, u32[]{:S(2)}, u32[]{:S(2)}) collective-permute-start(f32[4,8,128]{2,1,0:T(8,128)S(1)} %squares.3), channel_id=1, source_target_pairs={{0,1},{1,0},{2,3},{3,2},{4,5},{5,4},{6,7},{7,6},{8,9},{9,8},{10,11... | collective-permute-start | bytes 49160 | tf_op jit(solution)/shard_map/ppermute | solution.py:201
  62.2 5.2 %collective-permute-start.3 = (f32[4,8,128]{2,1,0:T(8,128)S(1)}, f32[4,8,128]{2,1,0:T(8,128)S(1)}, u32[]{:S(2)}, u32[]{:S(2)}) collective-permute-start(f32[4,8,128]{2,1,0:T(8,128)S(1)} %bitcast.17), channel_id=1, source_target_pairs={{0,1},{1,0},{2,3},{3,2},{4,5},{5,4},{6,7},{7,6},{8,9},{9,8},{10,11... | collective-permute-start | bytes 49160 | tf_op jit(solution)/shard_map/ppermute | solution.py:201

commit v7 on v4

--- a/solution.py
+++ b/solution.py
@@ -253,9 +253,9 @@
     given = squares_of(1 - core, embedded, weights, groups)
     received = around(given, "core", 1)
     kept = squares_of(core, embedded, weights, groups)
-    plane = exchange(pair_for_each(kept, received, lax.axis_size(PLANE)), PLANE)
-    column = exchange(sum_for_each(plane, lax.axis_size(COLUMN)), COLUMN)
-    totals = sum_for_each(column, 1)[0]
+    column = exchange(pair_for_each(kept, received, lax.axis_size(COLUMN)), COLUMN)
+    plane = exchange(sum_for_each(column, lax.axis_size(PLANE)), PLANE)
+    totals = sum_for_each(plane, 1)[0]
     others = around(totals, "core", 1)
     made = scaled_adapters(core, weights, embedded, totals, gain)
     made = scaled_adapters(1 - core, weights, embedded, others, gain, made)

time: 69.9 us -> 70.2 us (level)
  no operation moved by 1% of the time
where the time goes in v7:
time: 70.2 us; the launch traced here: 69.9 us
  blocking collectives  36 us (51%)
  starting transfers between devices  17.7 us (25%)
  Pallas kernels  11.6 us (17%)
  waiting for transfers between devices  4.53 us (6%)
    all_to_all x2, blocking collectives, exchange(): return lax.all_to_all(x, axis, split_axis=0, concat_axis=0, tiled=True)  24.3 us
    all_to_all x1, starting transfers between devices, exchange(): return lax.all_to_all(x, axis, split_axis=0, concat_axis=0, tiled=True)  11.9 us
    all_gather x1, blocking collectives, on_device(): ids = lax.all_gather(task_ids.reshape(1, -1), TASK, axis=0, tiled=True)  11.8 us
    pallas_call x2, Pallas kernels, scaled_adapters(): pl.pallas_call(kernel, out_shape=jax.ShapeDtypeStruct((groups * columns,...  4.52 us
    all_to_all x1, waiting for transfers between devices, exchange(): return lax.all_to_all(x, axis, split_axis=0, concat_axis=0, tiled=True)  4.52 us
    ppermute x2, starting transfers between devices, around(): return lax.ppermute(x, axis, [(i, (i + ahead) % size) for i in range(size)])  3.37 us
    ppermute x1, starting transfers between devices, on_device(): other = lax.ppermute(mine, 'core', [(0, 1), (1, 0)])  2.43 us
    pallas_call x2, Pallas kernels, squares_of(): pl.pallas_call(kernel, out_shape=jax.ShapeDtypeStruct((chunks, groups, LA...  2.4 us
  transfers between devices with their start and end apart: 4, of which 1 were waited for; matrix products, arithmetic and copies ran while one was open for 0% of the time, Pallas kernels for 7%

profile of v7, /device:TPU:1, one launch (start us, length us, event | category | flops | bytes accessed | tf_op | source)
XLA Modules:
  0.0 69.9 jit_solution(18003081199166669939)
XLA Ops:
  0.0 0.0 copy-start
  0.0 2.2 %encode_half.1 = bf16[32,32,256]{2,1,0:T(8,128)(2,1)} custom-call(s32[1]{0:T(128)} %bitcast.core_ref.side_ref, bf16[64,256]{1,0:T(8,128)(2,1)} %table_hbm.1, bf16[256,512]{1,0:T(8,128)(2,1)} %enc_in_hbm.1, bf16[512,256]{1,0:T(8,128)(2,1)} %enc_out_hbm.1), custom_call_target="tpu_custom_call" | custom-call | tf_op jit(solution)/shard_map/encode_half/pallas_call | solution.py:63
  2.3 11.9 %all-to-all-start = ((bf16[32,32,256]{2,1,0:T(8,128)(2,1)}), bf16[32,32,256]{2,1,0:T(8,128)(2,1)S(1)}, u32[]{:S(2)}, u32[]{:S(2)}) async-start(bf16[32,32,256]{2,1,0:T(8,128)(2,1)} %encode_half.1), calls=%async_computation | async-start | bytes 1048576 | tf_op jit(solution)/shard_map/all_to_all | solution.py:33
  14.1 11.8 %all-gather.1 = s32[8,1,128]{2,1,0:T(1,128)S(1)} all-gather(s32[1,1,128]{2,1,0:T(1,128)} %bitcast.18), channel_id=2, replica_groups=mesh['z'=8,'x'=4,'y'=4,'core'=2] {'y','core'}, dimensions={0}, use_global_device_ids=true | all-gather | bytes 4608 | tf_op jit(solution)/shard_map/all_gather | solution.py:248
  25.9 4.5 %all-to-all-done = bf16[32,32,256]{2,1,0:T(8,128)(2,1)S(1)} async-done(((bf16[32,32,256]{2,1,0:T(8,128)(2,1)}), bf16[32,32,256]{2,1,0:T(8,128)(2,1)S(1)}, u32[]{:S(2)}, u32[]{:S(2)}) %all-to-all-start) | async-done | bytes 524320 | tf_op jit(solution)/shard_map/all_to_all | solution.py:33
  30.4 2.4 %collective-permute-start = (bf16[1024,256]{1,0:T(8,128)(2,1)S(1)}, bf16[1024,256]{1,0:T(8,128)(2,1)S(1)}, u32[]{:S(2)}, u32[]{:S(2)}) collective-permute-start(bf16[1024,256]{1,0:T(8,128)(2,1)S(1)} %bitcast.11), channel_id=1, source_target_pairs={{0,1},{1,0},{2,3},{3,2},{4,5},{5,4},{6,7},{7,6},{8,9},{9,8},{10,11... | collective-permute-start | bytes 1572872 | tf_op jit(solution)/shard_map/ppermute | solution.py:250
  32.8 1.5 %first_half.1 = (bf16[1024,256]{1,0:T(8,128)(2,1)S(1)}, bf16[3584,256]{1,0:T(8,128)(2,1)S(1)}) custom-call(s32[1]{0:T(128)} %bitcast.core_ref.side_ref, s32[8,128]{1,0:T(8,128)S(1)} %bitcast.15, bf16[1024,256]{1,0:T(8,128)(2,1)S(1)} %bitcast.12, bf16[3584,256]{1,0:T(8,128)(2,1)} %bitcast.17), custom_call_target="tpu_custom_call" | custom-call | tf_op jit(solution)/shard_map/first_half/pallas_call | solution.py:95
  34.4 0.0 collective-permute-done.other_ref
  34.4 0.8 %embed.1.embedded_ref = bf16[1024,256]{1,0:T(8,128)(2,1)S(1)} custom-call(s32[1]{0:T(128)} %bitcast.core_ref.side_ref, s32[8,128]{1,0:T(8,128)S(1)} %bitcast.16, bf16[1024,256]{1,0:T(8,128)(2,1)S(1)} %get-tuple-element.16.part_ref, bf16[1024,256]{1,0:T(8,128)(2,1)S(1)} %collective-permute-done.other_ref), custom_call_target="tpu_custom_call" | custom-call | tf_op jit(solution)/shard_map/embed/pallas_call | solution.py:114
  35.2 1.2 %squares.3 = f32[4,8,128]{2,1,0:T(8,128)S(1)} custom-call(s32[1]{0:T(128)S(6)} %sub.4.side_ref, bf16[1024,256]{1,0:T(8,128)(2,1)S(1)} %embed.1.embedded_ref, bf16[3584,256]{1,0:T(8,128)(2,1)S(1)} %get-tuple-element.15.weights_ref), custom_call_target="tpu_custom_call" | custom-call | tf_op jit(solution)/shard_map/squares/pallas_call | solution.py:142
  36.4 0.5 collective-permute-start.1
  36.9 1.2 %squares.2.kept_ref = f32[4,8,128]{2,1,0:T(8,128)S(1)} custom-call(s32[1]{0:T(128)} %bitcast.core_ref.side_ref, bf16[1024,256]{1,0:T(8,128)(2,1)S(1)} %embed.1.embedded_ref, bf16[3584,256]{1,0:T(8,128)(2,1)S(1)} %get-tuple-element.15.weights_ref), custom_call_target="tpu_custom_call" | custom-call | tf_op jit(solution)/shard_map/squares/pallas_call | solution.py:142
  38.1 0.0 collective-permute-done.1.received_ref
  38.1 11.1 %all_to_all.15.pieces_ref = f32[8,4,8,128]{3,2,1,0:T(8,128)S(1)} all-to-all(f32[8,4,8,128]{3,2,1,0:T(8,128)S(1)} %pair_for_each.1), channel_id=1, replica_groups=mesh['z'=8,'x'=4,'y'=4,'core'=2] {'z'}, dimensions={0} | all-to-all | bytes 262144 | tf_op jit(solution)/shard_map/all_to_all | solution.py:33
  49.3 13.2 %all_to_all.16.pieces_ref = f32[16,4,8,128]{3,2,1,0:T(8,128)S(1)} all-to-all(f32[16,4,8,128]{3,2,1,0:T(8,128)S(1)} %sum_for_each.2), channel_id=1, replica_groups=mesh['z'=8,'x'=4,'y'=4,'core'=2] {'x','y'}, dimensions={0} | all-to-all | bytes 524288 | tf_op jit(solution)/shard_map/all_to_all | solution.py:33
  62.4 2.9 %collective-permute-start.2 = (f32[4,8,128]{2,1,0:T(8,128)S(1)}, f32[4,8,128]{2,1,0:T(8,128)S(1)}, u32[]{:S(2)}, u32[]{:S(2)}) collective-permute-start(f32[4,8,128]{2,1,0:T(8,128)S(1)} %bitcast.13), channel_id=1, source_target_pairs={{0,1},{1,0},{2,3},{3,2},{4,5},{5,4},{6,7},{7,6},{8,9},{9,8},{10,11... | collective-permute-start | bytes 49160 | tf_op jit(solution)/shard_map/ppermute | solution.py:188
  65.4 0.0 copy-done
  65.4 2.3 %scale.2.refs_0_ = bf16[3584,1024]{1,0:T(8,128)(2,1)} custom-call(s32[1]{0:T(128)} %bitcast.core_ref.side_ref, bf16[3584,256]{1,0:T(8,128)(2,1)S(1)} %get-tuple-element.15.weights_ref, bf16[1024,256]{1,0:T(8,128)(2,1)S(1)} %embed.1.embedded_ref, f32[4,8,128]{2,1,0:T(8,128)S(1)} %bitcast.14, bf16[8,448]{1,0:T(8,128)(2,1)S(1)} %copy-done), custom_call_target="tpu_custom_call" | custom-call | tf_op jit(solution)/shard_map/scale/pallas_call | solution.py:228
  67.6 0.0 collective-permute-done.2.totals_ref
  67.6 2.3 %scale.3 = bf16[3584,1024]{1,0:T(8,128)(2,1)} custom-call(s32[1]{0:T(128)S(6)} %sub.4.side_ref, bf16[3584,256]{1,0:T(8,128)(2,1)S(1)} %get-tuple-element.15.weights_ref, bf16[1024,256]{1,0:T(8,128)(2,1)S(1)} %embed.1.embedded_ref, f32[4,8,128]{2,1,0:T(8,128)S(1)} %collective-permute-done.2.totals_ref, ...), custom_call_target="tpu_custom_call", output_to_operand_aliasing={{}: (5, {})} | custom-call | tf_op jit(solution)/shard_map/scale/pallas_call | solution.py:228
  (3 shorter events, 0.1 us)
Async XLA Ops:
  0.0 65.4 %copy-start = (bf16[8,448]{1,0:T(8,128)(2,1)S(1)}, bf16[8,448]{1,0:T(8,128)(2,1)}, u32[]{:S(2)}) copy-start(bf16[8,448]{1,0:T(8,128)(2,1)} %gain_ref.3) | copy-start | bytes 21508
  2.3 28.2 %all-to-all-start = ((bf16[32,32,256]{2,1,0:T(8,128)(2,1)}), bf16[32,32,256]{2,1,0:T(8,128)(2,1)S(1)}, u32[]{:S(2)}, u32[]{:S(2)}) async-start(bf16[32,32,256]{2,1,0:T(8,128)(2,1)} %encode_half.1), calls=%async_computation | async-start | bytes 1048576 | tf_op jit(solution)/shard_map/all_to_all | solution.py:33
  30.4 4.0 %collective-permute-start = (bf16[1024,256]{1,0:T(8,128)(2,1)S(1)}, bf16[1024,256]{1,0:T(8,128)(2,1)S(1)}, u32[]{:S(2)}, u32[]{:S(2)}) collective-permute-start(bf16[1024,256]{1,0:T(8,128)(2,1)S(1)} %bitcast.11), channel_id=1, source_target_pairs={{0,1},{1,0},{2,3},{3,2},{4,5},{5,4},{6,7},{7,6},{8,9},{9,8},{10,11... | collective-permute-start | bytes 1572872 | tf_op jit(solution)/shard_map/ppermute | solution.py:250
  36.4 1.7 %collective-permute-start.1 = (f32[4,8,128]{2,1,0:T(8,128)S(1)}, f32[4,8,128]{2,1,0:T(8,128)S(1)}, u32[]{:S(2)}, u32[]{:S(2)}) collective-permute-start(f32[4,8,128]{2,1,0:T(8,128)S(1)} %squares.3), channel_id=1, source_target_pairs={{0,1},{1,0},{2,3},{3,2},{4,5},{5,4},{6,7},{7,6},{8,9},{9,8},{10,11... | collective-permute-start | bytes 49160 | tf_op jit(solution)/shard_map/ppermute | solution.py:188
  62.4 5.2 %collective-permute-start.2 = (f32[4,8,128]{2,1,0:T(8,128)S(1)}, f32[4,8,128]{2,1,0:T(8,128)S(1)}, u32[]{:S(2)}, u32[]{:S(2)}) collective-permute-start(f32[4,8,128]{2,1,0:T(8,128)S(1)} %bitcast.13), channel_id=1, source_target_pairs={{0,1},{1,0},{2,3},{3,2},{4,5},{5,4},{6,7},{7,6},{8,9},{9,8},{10,11... | collective-permute-start | bytes 49160 | tf_op jit(solution)/shard_map/ppermute | solution.py:188
